TPU v7x, 256 devices: a whole 4x4x8 slice. The times are simulated.
256 devices in a mesh: tm: 128 (over y_hi, z, x, core), mom: 2 (over y_lo).
Axes of the slice: x: 4, y: 4 (y_hi: 2, y_lo: 2; y = y_hi * 2 + y_lo), z: 8, core: 2. Of those that a mesh axis runs over, the one named last changes fastest.
Arguments:
- fields: bfloat16 [128, 4, 2, 512, 512], P('tm', 'mom'), may hold values from -1 to 1
- mom_pairs: int32 [6, 2], P('mom'), may hold values from 0 to 3, as said below
- deltas: int32 [4], replicated, may hold values from 0 to 3, each once
Outputs:
- time_traces: float32 [128, 2, 4, 6], P('tm', None, None, 'mom')
- summed_traces: float32 [2, 4, 6], P(None, None, 'mom')
Inputs may be any that keep to these rules, and one draw needn't show every extreme that they name: `mom_pairs`: column 0 may be any momentum; in row r, column 1 lies in momentum group r // 3, that is from (r // 3) * 2 to (r // 3) * 2 + 1.
All inputs are finite; a program needn't handle non-finite values.
Results may differ from a plain program's by a relative error of at most 0.0003.
Values may be sent and summed in bfloat16 or wider, within the bound.
A program may use at most 128 MiB of HBM per device.

v0:
```python
import jax
import jax.numpy as jnp
from jax import lax
from jax.sharding import Mesh
from jax.sharding import PartitionSpec as P

TM = ("tm_0", "tm_1", "tm_2", "tm_3")


def sent_to_all(array, axis):
    copies = jnp.broadcast_to(array, (lax.axis_size(axis), *array.shape))
    return lax.all_to_all(copies, axis, split_axis=0, concat_axis=0, tiled=True)


def joined_along(tiles, dim):
    dims = list(tiles.shape[1:])
    dims[dim] *= tiles.shape[0]
    return jnp.moveaxis(tiles, 0, dim).reshape(dims)


def collect(array, axis, dim):
    tiles = sent_to_all(array, axis)
    return joined_along(tiles, dim)


def over_axes(array, axes):
    for axis in axes:
        array = lax.psum(array, axis)
    return array


def from_behind(block, axis, distance):
    devices = range(lax.axis_size(axis))
    route = [((i - distance) % len(devices), i) for i in devices]
    return lax.ppermute(block, axis, route)


def products(source, target):
    product_full = jnp.einsum("xij,yjk->xyik", source, target, preferred_element_type=jnp.float32)
    real_part = product_full[0, 0] - product_full[1, 1]
    imag_part = product_full[0, 1] + product_full[1, 0]
    direct = jnp.trace(real_part)
    box_value = jnp.sum(real_part * real_part.T) - jnp.sum(imag_part * imag_part.T)
    return (direct, box_value)


def pair_terms(source_stack, target_stack, target_index):
    directs = []
    boxes = []
    for which in range(source_stack.shape[0]):
        target = lax.dynamic_index_in_dim(target_stack, target_index[which], 0, keepdims=False)
        direct, box_value = products(source_stack[which], target)
        directs.append(direct)
        boxes.append(box_value)
    return jnp.stack([jnp.stack(directs), jnp.stack(boxes)])


def reorder(stacked, deltas):
    picker = (deltas[:, None] == jnp.arange(deltas.shape[0], dtype=jnp.int32)[None, :]).astype(
        jnp.float32
    )
    return jnp.sum(picker[:, :, None] * stacked[..., None, :, :], axis=-2)


def per_device(fields, mom_pairs, deltas):
    group_index = lax.axis_index("mom")
    per_group = fields.shape[1]
    sep_count = deltas.shape[0]
    own_fields = fields[0]
    all_momenta = collect(own_fields, "mom", 0)
    pair_count = mom_pairs.shape[0]
    sources = jnp.stack(
        [
            lax.dynamic_index_in_dim(all_momenta, mom_pairs[which, 0], 0, keepdims=False)
            for which in range(pair_count)
        ]
    )
    target_index = mom_pairs[:, 1] - group_index * per_group
    raw_terms = []
    local_terms = []
    totals = []

    def record(result):
        totals.append(over_axes(result, TM))
        raw_terms.append(result)

    moving = own_fields
    for separation in range(1, sep_count + 1):
        moving = from_behind(moving, TM, -1)
        result = pair_terms(sources, moving, target_index)
        record(result)
        local_terms.append(result)
    time_traces = reorder(jnp.stack(local_terms, axis=1), deltas)[None]
    summed = jnp.stack(totals, axis=1)
    summed_traces = reorder(summed, deltas)
    return (time_traces, summed_traces)


def solution(mesh):
    finer = Mesh(
        mesh.devices.reshape(2, 8, 4, 2, mesh.shape["mom"]), ("tm_0", "tm_1", "tm_2", "tm_3", "mom")
    )
    in_specs = (P(TM, "mom", None, None, None), P("mom", None), P())
    out_specs = (P(TM, None, None, "mom"), P(None, None, "mom"))
    return jax.shard_map(
        per_device, mesh=finer, in_specs=in_specs, out_specs=out_specs, check_vma=False
    )
```

profile of v0, /device:TPU:1, one launch (start us, length us, event | category | flops | bytes accessed | tf_op | source)
XLA Modules:
  0.0 271.7 jit_solution(15614361665262822510)
XLA Ops:
  0.6 3.9 %broadcast_in_dim.27 = bf16[2,2,2,512,512]{4,3,2,1,0:T(8,128)(2,1)} broadcast(bf16[2,2,512,512]{3,2,1,0:T(8,128)(2,1)} %bitcast.329), dimensions={1,2,3,4} | broadcast | bytes 6291456 | tf_op jit(solution)/shard_map/broadcast_in_dim | solution.py:11
  4.6 5.7 %all-to-all-start = ((bf16[2,2,2,512,512]{4,3,2,1,0:T(8,128)(2,1)}), bf16[2,2,2,512,512]{4,3,2,1,0:T(8,128)(2,1)}, u32[]{:S(2)}, u32[]{:S(2)}) async-start(bf16[2,2,2,512,512]{4,3,2,1,0:T(8,128)(2,1)} %broadcast_in_dim.27), calls=%async_computation | async-start | bytes 8388608 | tf_op jit(solution)/shard_map/all_to_all | solution.py:12
  10.3 3.3 %collective-permute-start = (bf16[2,2,512,512]{3,2,1,0:T(8,128)(2,1)}, bf16[2,2,512,512]{3,2,1,0:T(8,128)(2,1)S(1)}, u32[]{:S(2)}, u32[]{:S(2)}) collective-permute-start(bf16[2,2,512,512]{3,2,1,0:T(8,128)(2,1)} %bitcast.330), channel_id=1, source_target_pairs={{2,0},{4,2},{6,4},{8,6},{10,8},{12,10},{14,12},{16,14},{18,16},{20... | collective-permute-start | bytes 6291464 | tf_op jit(solution)/shard_map/ppermute | solution.py:35
  25.9 29.9 %all-to-all-done = bf16[2,2,2,512,512]{4,3,2,1,0:T(8,128)(2,1)} async-done(((bf16[2,2,2,512,512]{4,3,2,1,0:T(8,128)(2,1)}), bf16[2,2,2,512,512]{4,3,2,1,0:T(8,128)(2,1)}, u32[]{:S(2)}, u32[]{:S(2)}) %all-to-all-start) | async-done | bytes 4194336 | tf_op jit(solution)/shard_map/all_to_all | solution.py:12
  62.8 4.0 %collective-permute-start.1 = (bf16[2,2,512,512]{3,2,1,0:T(8,128)(2,1)}, bf16[2,2,512,512]{3,2,1,0:T(8,128)(2,1)}, u32[]{:S(2)}, u32[]{:S(2)}) collective-permute-start(bf16[2,2,512,512]{3,2,1,0:T(8,128)(2,1)} %copy-done.9), channel_id=1, source_target_pairs={{2,0},{4,2},{6,4},{8,6},{10,8},{12,10},{14,12},{16,14},{18,16},{20... | collective-permute-start | bytes 6291464 | tf_op jit(solution)/shard_map/ppermute | solution.py:35
  71.1 2.9 %copy.61 = f32[512,512]{1,0:T(8,128)} copy(f32[512,512]{0,1:T(8,128)} %get-tuple-element.49) | data formatting | bytes 2097152 | tf_op jit(solution)/shard_map/sub | solution.py:40
  75.3 2.8 %convolution_bitcast_fusion.9 = f32[2,2,512,512]{2,3,1,0:T(8,128)S(1)} fusion(bf16[2,2,512,512]{3,2,1,0:T(8,128)(2,1)} %copy-done.9, s32[]{:T(128)S(6)} %select_n.73, bf16[4,2,512,512]{3,2,1,0:T(8,128)(2,1)} %bitcast.5, s32[]{:T(128)S(6)} %select_n.74), kind=kOutput, calls=%fused_computation.9 | convolution fusion | flops 1073741824 | bytes 6291464 | tf_op jit(solution)/shard_map/xij,yjk->xyik/dot_general | solution.py:39
  85.6 3.4 %select_reduce_fusion.10 = (f32[]{:T(128)}, f32[]{:T(128)}, f32[]{:T(128)}) fusion(f32[512,512]{0,1:T(8,128)} %get-tuple-element.49, f32[512,512]{1,0:T(8,128)} %copy.61, f32[512,512]{0,1:T(8,128)} %copy-done.4, f32[512,512]{1,0:T(8,128)} %copy.62), kind=kLoop, calls=%fused_computation.152 | loop fusion | flops 1835005 | bytes 4194316 | tf_op jit(solution)/shard_map/jit(trace)/reduce_sum | solution.py:42
  96.0 2.8 %convolution_bitcast_fusion.8 = f32[2,2,512,512]{2,3,1,0:T(8,128)S(1)} fusion(bf16[2,2,512,512]{3,2,1,0:T(8,128)(2,1)} %collective-permute-done.1, s32[]{:T(128)S(6)} %select_n.67, bf16[4,2,512,512]{3,2,1,0:T(8,128)(2,1)} %bitcast.5, s32[]{:T(128)S(6)} %select_n.68), kind=kOutput, calls=%fused_computation.8 | convolution fusion | flops 1073741824 | bytes 6291464 | tf_op jit(solution)/shard_map/xij,yjk->xyik/dot_general | solution.py:39
  102.0 32.1 %collective-permute-start.2 = (bf16[2,2,512,512]{3,2,1,0:T(8,128)(2,1)}, bf16[2,2,512,512]{3,2,1,0:T(8,128)(2,1)}, u32[]{:S(2)}, u32[]{:S(2)}) collective-permute-start(bf16[2,2,512,512]{3,2,1,0:T(8,128)(2,1)} %collective-permute-done.1), channel_id=1, source_target_pairs={{2,0},{4,2},{6,4},{8,6},{10,8},{12,10},{14,12},{16,14},{18,16},{20... | collective-permute-start | bytes 6291464 | tf_op jit(solution)/shard_map/ppermute | solution.py:35
  138.4 2.9 %copy.73 = f32[512,512]{1,0:T(8,128)} copy(f32[512,512]{0,1:T(8,128)} %get-tuple-element.55) | data formatting | bytes 2097152 | tf_op jit(solution)/shard_map/sub | solution.py:40
  152.9 3.4 %select_reduce_fusion.7 = (f32[]{:T(128)}, f32[]{:T(128)}, f32[]{:T(128)}) fusion(f32[512,512]{0,1:T(8,128)} %get-tuple-element.55, f32[512,512]{1,0:T(8,128)} %copy.73, f32[512,512]{0,1:T(8,128)} %copy-done.5, f32[512,512]{1,0:T(8,128)} %copy.74), kind=kLoop, calls=%fused_computation.146 | loop fusion | flops 1835005 | bytes 4194316 | tf_op jit(solution)/shard_map/jit(trace)/reduce_sum | solution.py:42
  163.2 2.8 %convolution_bitcast_fusion.5 = f32[2,2,512,512]{2,3,1,0:T(8,128)S(1)} fusion(bf16[2,2,512,512]{3,2,1,0:T(8,128)(2,1)} %collective-permute-done.2, s32[]{:T(128)S(6)} %select_n.67, bf16[4,2,512,512]{3,2,1,0:T(8,128)(2,1)} %bitcast.5, s32[]{:T(128)S(6)} %select_n.68), kind=kOutput, calls=%fused_computation.5 | convolution fusion | flops 1073741824 | bytes 6291464 | tf_op jit(solution)/shard_map/xij,yjk->xyik/dot_general | solution.py:39
  171.8 2.8 %convolution_bitcast_fusion.4 = f32[2,2,512,512]{2,3,1,0:T(8,128)S(1)} fusion(bf16[2,2,512,512]{3,2,1,0:T(8,128)(2,1)} %collective-permute-done.2, s32[]{:T(128)S(6)} %select_n.70, bf16[4,2,512,512]{3,2,1,0:T(8,128)(2,1)} %bitcast.5, s32[]{:T(128)S(6)} %select_n.71), kind=kOutput, calls=%fused_computation.4 | convolution fusion | flops 1073741824 | bytes 6291464 | tf_op jit(solution)/shard_map/xij,yjk->xyik/dot_general | solution.py:39
  176.1 2.9 %copy.85 = f32[512,512]{1,0:T(8,128)} copy(f32[512,512]{0,1:T(8,128)} %get-tuple-element.61) | data formatting | bytes 2097152 | tf_op jit(solution)/shard_map/sub | solution.py:40
  180.3 2.8 %convolution_bitcast_fusion.3 = f32[2,2,512,512]{2,3,1,0:T(8,128)S(1)} fusion(bf16[2,2,512,512]{3,2,1,0:T(8,128)(2,1)} %collective-permute-done.2, s32[]{:T(128)S(6)} %select_n.73, bf16[4,2,512,512]{3,2,1,0:T(8,128)(2,1)} %bitcast.5, s32[]{:T(128)S(6)} %select_n.74), kind=kOutput, calls=%fused_computation.3 | convolution fusion | flops 1073741824 | bytes 6291464 | tf_op jit(solution)/shard_map/xij,yjk->xyik/dot_general | solution.py:39
  190.6 3.4 %select_reduce_fusion.4 = (f32[]{:T(128)}, f32[]{:T(128)}, f32[]{:T(128)}) fusion(f32[512,512]{0,1:T(8,128)} %get-tuple-element.61, f32[512,512]{1,0:T(8,128)} %copy.85, f32[512,512]{0,1:T(8,128)} %copy-done.6, f32[512,512]{1,0:T(8,128)} %copy.86), kind=kLoop, calls=%fused_computation.140 | loop fusion | flops 1835005 | bytes 4194316 | tf_op jit(solution)/shard_map/jit(trace)/reduce_sum | solution.py:42
  201.0 2.8 %convolution_bitcast_fusion.2 = f32[2,2,512,512]{2,3,1,0:T(8,128)S(1)} fusion(bf16[2,2,512,512]{3,2,1,0:T(8,128)(2,1)} %collective-permute-done.3, s32[]{:T(128)S(6)} %select_n.67, bf16[4,2,512,512]{3,2,1,0:T(8,128)(2,1)} %bitcast.5, s32[]{:T(128)S(6)} %select_n.68), kind=kOutput, calls=%fused_computation.2 | convolution fusion | flops 1073741824 | bytes 6291464 | tf_op jit(solution)/shard_map/xij,yjk->xyik/dot_general | solution.py:39
  206.9 2.8 %convolution_bitcast_fusion.1 = f32[2,2,512,512]{2,3,1,0:T(8,128)S(1)} fusion(bf16[2,2,512,512]{3,2,1,0:T(8,128)(2,1)} %collective-permute-done.3, s32[]{:T(128)S(6)} %select_n.70, bf16[4,2,512,512]{3,2,1,0:T(8,128)(2,1)} %bitcast.5, s32[]{:T(128)S(6)} %select_n.71), kind=kOutput, calls=%fused_computation.1 | convolution fusion | flops 1073741824 | bytes 6291464 | tf_op jit(solution)/shard_map/xij,yjk->xyik/dot_general | solution.py:39
  215.2 2.8 %convolution_bitcast_fusion = f32[2,2,512,512]{2,3,1,0:T(8,128)S(1)} fusion(bf16[2,2,512,512]{3,2,1,0:T(8,128)(2,1)} %collective-permute-done.3, s32[]{:T(128)S(6)} %select_n.73, bf16[4,2,512,512]{3,2,1,0:T(8,128)(2,1)} %bitcast.5, s32[]{:T(128)S(6)} %select_n.74), kind=kOutput, calls=%fused_computation | convolution fusion | flops 1073741824 | bytes 6291464 | tf_op jit(solution)/shard_map/xij,yjk->xyik/dot_general | solution.py:39
  237.3 5.3 %all-reduce.3 = (f32[2,3]{1,0:T(2,128)S(1)}, f32[2,3]{1,0:T(2,128)S(1)}, f32[2,3]{1,0:T(2,128)S(1)}, f32[2,3]{1,0:T(2,128)S(1)}) all-reduce(f32[2,3]{1,0:T(2,128)S(1)} %get-tuple-element.77, f32[2,3]{1,0:T(2,128)S(1)} %get-tuple-element.75, ...), channel_id=1, replica_groups=mesh['tm_0'=2,'tm_1'=8,'tm_2'=4,'tm_3'=2,'mom'=2] {'tm_0'}, use_global_device_ids=true, to_apply=%region_49.50 | all-reduce | flops 24 | bytes 192 | tf_op jit(solution)/shard_map/psum | solution.py:28
  242.5 10.9 %all-reduce = (f32[2,3]{1,0:T(2,128)S(1)}, f32[2,3]{1,0:T(2,128)S(1)}, f32[2,3]{1,0:T(2,128)S(1)}, f32[2,3]{1,0:T(2,128)S(1)}) all-reduce(f32[2,3]{1,0:T(2,128)S(1)} %get-tuple-element.42, f32[2,3]{1,0:T(2,128)S(1)} %get-tuple-element.43, ...), channel_id=1, replica_groups=mesh['tm_0'=2,'tm_1'=8,'tm_2'=4,'tm_3'=2,'mom'=2] {'tm_1'}, use_global_device_ids=true, to_apply=%region_50.51 | all-reduce | flops 24 | bytes 192 | tf_op jit(solution)/shard_map/psum | solution.py:28
  253.4 7.7 %all-reduce.1 = (f32[2,3]{1,0:T(2,128)S(1)}, f32[2,3]{1,0:T(2,128)S(1)}, f32[2,3]{1,0:T(2,128)S(1)}, f32[2,3]{1,0:T(2,128)S(1)}) all-reduce(f32[2,3]{1,0:T(2,128)S(1)} %get-tuple-element.30, f32[2,3]{1,0:T(2,128)S(1)} %get-tuple-element.31, ...), channel_id=1, replica_groups=mesh['tm_0'=2,'tm_1'=8,'tm_2'=4,'tm_3'=2,'mom'=2] {'tm_2'}, use_global_device_ids=true, to_apply=%region_51.52 | all-reduce | flops 24 | bytes 192 | tf_op jit(solution)/shard_map/psum | solution.py:28
  261.1 9.0 %all-reduce.2 = (f32[2,1,3]{2,0,1:T(2,128)S(1)}, f32[2,1,3]{2,0,1:T(2,128)S(1)}, f32[2,1,3]{2,0,1:T(2,128)S(1)}, f32[2,1,3]{2,0,1:T(2,128)S(1)}) all-reduce(f32[2,1,3]{2,0,1:T(2,128)S(1)} %bitcast.332, f32[2,1,3]{2,0,1:T(2,128)S(1)} %bitcast.333, ...), channel_id=1, replica_groups=mesh['tm_0'=2,'tm_1'=8,'tm_2'=4,'tm_3'=2,'mom'=2] {'tm_3'}, use_global_device_ids=true, to_apply=%region_52.53 | all-reduce | flops 24 | bytes 192 | tf_op jit(solution)/shard_map/psum | solution.py:28
  (110 shorter events, 90.4 us)
Async XLA Ops:
  4.6 9.0 %copy-start.16 = (s32[3,2]{0,1:T(2,128)S(1)}, s32[3,2]{0,1:T(2,128)}, u32[]{:S(2)}) copy-start(s32[3,2]{0,1:T(2,128)} %param.4) | copy-start | bytes 76
  4.6 21.3 %copy-start.17 = (s32[4]{0:T(128)S(1)}, s32[4]{0:T(128)}, u32[]{:S(2)}) copy-start(s32[4]{0:T(128)} %param.5) | copy-start | bytes 52
  4.6 51.2 %all-to-all-start = ((bf16[2,2,2,512,512]{4,3,2,1,0:T(8,128)(2,1)}), bf16[2,2,2,512,512]{4,3,2,1,0:T(8,128)(2,1)}, u32[]{:S(2)}, u32[]{:S(2)}) async-start(bf16[2,2,2,512,512]{4,3,2,1,0:T(8,128)(2,1)} %broadcast_in_dim.27), calls=%async_computation | async-start | bytes 8388608 | tf_op jit(solution)/shard_map/all_to_all | solution.py:12
  10.3 45.5 %collective-permute-start = (bf16[2,2,512,512]{3,2,1,0:T(8,128)(2,1)}, bf16[2,2,512,512]{3,2,1,0:T(8,128)(2,1)S(1)}, u32[]{:S(2)}, u32[]{:S(2)}) collective-permute-start(bf16[2,2,512,512]{3,2,1,0:T(8,128)(2,1)} %bitcast.330), channel_id=1, source_target_pairs={{2,0},{4,2},{6,4},{8,6},{10,8},{12,10},{14,12},{16,14},{18,16},{20... | collective-permute-start | bytes 6291464 | tf_op jit(solution)/shard_map/ppermute | solution.py:35
  55.8 1.3 copy-start.9
  60.2 9.5 %copy-start = (f32[512,512]{0,1:T(8,128)}, f32[512,512]{0,1:T(8,128)S(1)}, u32[]{:S(2)}) copy-start(f32[512,512]{0,1:T(8,128)S(1)} %get-tuple-element.47) | copy-start | bytes 3145732
  62.8 33.1 %collective-permute-start.1 = (bf16[2,2,512,512]{3,2,1,0:T(8,128)(2,1)}, bf16[2,2,512,512]{3,2,1,0:T(8,128)(2,1)}, u32[]{:S(2)}, u32[]{:S(2)}) collective-permute-start(bf16[2,2,512,512]{3,2,1,0:T(8,128)(2,1)} %copy-done.9), channel_id=1, source_target_pairs={{2,0},{4,2},{6,4},{8,6},{10,8},{12,10},{14,12},{16,14},{18,16},{20... | collective-permute-start | bytes 6291464 | tf_op jit(solution)/shard_map/ppermute | solution.py:35
  71.1 4.2 %copy-start.4 = (f32[512,512]{0,1:T(8,128)}, f32[512,512]{0,1:T(8,128)S(1)}, u32[]{:S(2)}) copy-start(f32[512,512]{0,1:T(8,128)S(1)} %get-tuple-element.48) | copy-start | bytes 3145732
  84.2 6.0 %copy-start.10 = (f32[512,512]{1,0:T(8,128)S(1)}, f32[512,512]{1,0:T(8,128)}, u32[]{:S(2)}) copy-start(f32[512,512]{1,0:T(8,128)} %copy.63) | copy-start | bytes 3145732
  99.3 37.6 %copy-start.1 = (f32[512,512]{0,1:T(8,128)}, f32[512,512]{0,1:T(8,128)S(1)}, u32[]{:S(2)}) copy-start(f32[512,512]{0,1:T(8,128)S(1)} %get-tuple-element.53) | copy-start | bytes 3145732
  102.0 61.3 %collective-permute-start.2 = (bf16[2,2,512,512]{3,2,1,0:T(8,128)(2,1)}, bf16[2,2,512,512]{3,2,1,0:T(8,128)(2,1)}, u32[]{:S(2)}, u32[]{:S(2)}) collective-permute-start(bf16[2,2,512,512]{3,2,1,0:T(8,128)(2,1)} %collective-permute-done.1), channel_id=1, source_target_pairs={{2,0},{4,2},{6,4},{8,6},{10,8},{12,10},{14,12},{16,14},{18,16},{20... | collective-permute-start | bytes 6291464 | tf_op jit(solution)/shard_map/ppermute | solution.py:35
  138.4 4.2 %copy-start.5 = (f32[512,512]{0,1:T(8,128)}, f32[512,512]{0,1:T(8,128)S(1)}, u32[]{:S(2)}) copy-start(f32[512,512]{0,1:T(8,128)S(1)} %get-tuple-element.54) | copy-start | bytes 3145732
  151.5 6.0 %copy-start.11 = (f32[512,512]{1,0:T(8,128)S(1)}, f32[512,512]{1,0:T(8,128)}, u32[]{:S(2)}) copy-start(f32[512,512]{1,0:T(8,128)} %copy.75) | copy-start | bytes 3145732
  166.6 8.0 %copy-start.2 = (f32[512,512]{0,1:T(8,128)}, f32[512,512]{0,1:T(8,128)S(1)}, u32[]{:S(2)}) copy-start(f32[512,512]{0,1:T(8,128)S(1)} %get-tuple-element.59) | copy-start | bytes 3145732
  169.3 31.7 %collective-permute-start.3 = (bf16[2,2,512,512]{3,2,1,0:T(8,128)(2,1)}, bf16[2,2,512,512]{3,2,1,0:T(8,128)(2,1)}, u32[]{:S(2)}, u32[]{:S(2)}) collective-permute-start(bf16[2,2,512,512]{3,2,1,0:T(8,128)(2,1)} %collective-permute-done.2), channel_id=1, source_target_pairs={{2,0},{4,2},{6,4},{8,6},{10,8},{12,10},{14,12},{16,14},{18,16},{20... | collective-permute-start | bytes 6291464 | tf_op jit(solution)/shard_map/ppermute | solution.py:35
  176.1 4.2 %copy-start.6 = (f32[512,512]{0,1:T(8,128)}, f32[512,512]{0,1:T(8,128)S(1)}, u32[]{:S(2)}) copy-start(f32[512,512]{0,1:T(8,128)S(1)} %get-tuple-element.60) | copy-start | bytes 3145732
  189.2 6.0 %copy-start.12 = (f32[512,512]{1,0:T(8,128)S(1)}, f32[512,512]{1,0:T(8,128)}, u32[]{:S(2)}) copy-start(f32[512,512]{1,0:T(8,128)} %copy.87) | copy-start | bytes 3145732
  225.2 2.7 copy-start.3
  225.2 2.7 copy-start.13
  225.2 5.0 %copy-start.7 = (f32[512,512]{0,1:T(8,128)S(1)}, f32[512,512]{0,1:T(8,128)}, u32[]{:S(2)}) copy-start(f32[512,512]{0,1:T(8,128)} %get-tuple-element.68) | copy-start | bytes 3145732
  225.2 5.0 %copy-start.8 = (f32[512,512]{0,1:T(8,128)S(1)}, f32[512,512]{0,1:T(8,128)}, u32[]{:S(2)}) copy-start(f32[512,512]{0,1:T(8,128)} %get-tuple-element.69) | copy-start | bytes 3145732
  225.2 5.0 %copy-start.14 = (f32[512,512]{1,0:T(8,128)S(1)}, f32[512,512]{1,0:T(8,128)}, u32[]{:S(2)}) copy-start(f32[512,512]{1,0:T(8,128)} %copy.100) | copy-start | bytes 3145732
  225.2 5.0 %copy-start.15 = (f32[512,512]{1,0:T(8,128)S(1)}, f32[512,512]{1,0:T(8,128)}, u32[]{:S(2)}) copy-start(f32[512,512]{1,0:T(8,128)} %copy.99) | copy-start | bytes 3145732
where the time goes:
time: 277 us; the launch traced here: 272 us
  other arithmetic  51.2 us (18%)
  local copies, waits for them, and re-layouts  48.4 us (17%)
  starting transfers between devices  47.6 us (17%)
  matrix products  33.8 us (12%)
  blocking collectives  32.8 us (12%)
  waiting for transfers between devices  29.9 us (11%)
  between operations  28.1 us (10%)
    ppermute x4, starting transfers between devices, from_behind(): return lax.ppermute(block, axis, route)  41.9 us
    dot_general x12, matrix products, products(): jnp.einsum('xij,yjk->xyik', source, target, preferred_element_type=jnp.fl...  33.8 us
    psum x4, blocking collectives, over_axes(): array = lax.psum(array, axis)  32.8 us
    reduce_sum x12, other arithmetic, products(): direct = jnp.trace(real_part)  31.6 us
    all_to_all x1, waiting for transfers between devices, sent_to_all(): return lax.all_to_all(copies, axis, split_axis=0, concat_axis=0, tiled=True)  29.9 us
    sub x12, local copies, waits for them, and re-layouts, products(): real_part = product_full[0, 0] - product_full[1, 1]  23.2 us
    add x12, local copies, waits for them, and re-layouts, products(): imag_part = product_full[0, 1] + product_full[1, 0]  17.3 us
    add x12, other arithmetic, products(): imag_part = product_full[0, 1] + product_full[1, 0]  11.2 us
  transfers between devices with their start and end apart: 5, of which 1 were waited for; matrix products, arithmetic and copies ran while one was open for 28% of the time, Pallas kernels for 0%

commit v1 on v0

v1 whole, which is shorter than its diff:
```python
import functools

import jax
import jax.numpy as jnp
from jax import lax
from jax.experimental import pallas as pl
from jax.experimental.pallas import tpu as pltpu
from jax.sharding import PartitionSpec as P

MESH = pl.DeviceIdType.MESH
CHIPS_PER_PLANE = 32
ROWS = 128
CHUNKS = 4
SUB = 4
PIECES = CHUNKS * SUB
PIECE_ROWS = ROWS // SUB
NEV = ROWS * CHUNKS
PAIRS = 3
SEPS = 4


def place():
    time, group = lax.axis_index("tm"), lax.axis_index("mom")
    count = lax.axis_size("tm")
    chip, core = time // 2, time % 2
    swap_right = (chip % CHIPS_PER_PLANE) // (CHIPS_PER_PLANE - 1)
    swap_left = ((chip + 1) % CHIPS_PER_PLANE == 1).astype(jnp.int32)
    right = {"tm": (time + 2) % count, "mom": (group + swap_right) % 2}
    left = {"tm": (time + count - 2) % count, "mom": (group + swap_left) % 2}
    across = {"tm": time, "mom": 1 - group}
    partner = {"tm": time + 1 - 2 * core, "mom": group}
    return time, group, core, right, left, across, partner


def folded(values):
    total = values.reshape(-1, 8, values.shape[-1]).sum(0)
    lanes = [total[:, i : i + 128] for i in range(0, values.shape[-1], 128)]
    return functools.reduce(jnp.add, lanes)


def trace_kernel(
    pairs_own, pairs_sent, fields, tile,
    own, near, fed, ahead, source, wide, sums, flips, boxes, directs, rows_out, pairs_in, pairs_other,
    load_sem, pair_sems, near_sems, send_right, recv_right, send_left, recv_left, send_y, recv_y, send_core, recv_core,
):
    time, group, core, right, left, across, partner = place()
    from_left = left["mom"]
    from_right = right["mom"]

    def rows(j):
        return pl.ds(pl.multiple_of(j * PIECE_ROWS, PIECE_ROWS), PIECE_ROWS)

    def remote(src, dst, send, recv, device):
        return pltpu.make_async_remote_copy(
            src_ref=src, dst_ref=dst, send_sem=send, recv_sem=recv, device_id=device, device_id_type=MESH
        )

    def to_right(j):
        return remote(
            own.at[:, :, rows(j), :], source.at[group, :, :, rows(j), :], send_right.at[j], recv_right.at[j], right
        )

    def to_left(j):
        return remote(own.at[:, :, rows(j), :], ahead.at[:, :, rows(j), :], send_left.at[j], recv_left.at[j], left)

    def over_y(j):
        part = source.at[from_left, :, :, rows(j), :]
        return remote(part, part, send_y.at[j], recv_y.at[j], across)

    def feed_source(j):
        return remote(
            source.at[from_left, :, :, rows(j), :], fed.at[:, :, rows(j), :], send_core.at[j], recv_core.at[j], partner
        )

    def feed_ahead(j):
        return remote(ahead.at[:, :, rows(j), :], fed.at[:, :, rows(j), :], send_core.at[j], recv_core.at[j], partner)

    near_copy = remote(own, near, near_sems.at[0], near_sems.at[1], partner)
    pair_copy = remote(pairs_sent, pairs_in, pair_sems.at[0], pair_sems.at[1], across)
    load = pltpu.make_async_copy(fields, own, load_sem)

    barrier = pltpu.get_barrier_semaphore()
    load.start()
    for device in (right, left, across, partner):
        pl.semaphore_signal(barrier, inc=1, device_id=device, device_id_type=MESH)
    load.wait()
    pl.semaphore_wait(barrier, 4)

    @pl.when(core == 1)
    def _():
        @pl.loop(0, PIECES)
        def _(j):
            to_right(j).start()

    @pl.when(core == 0)
    def _():
        @pl.loop(0, PIECES)
        def _(j):
            to_left(j).start()

    pair_copy.start()
    near_copy.start()

    @pl.loop(0, SEPS * PAIRS)
    def _(i):
        boxes[i] = jnp.zeros((8, 128), jnp.float32)
        directs[i] = jnp.zeros((8, 128), jnp.float32)

        @pl.loop(0, NEV // 32)
        def _(r):
            at = pl.ds(pl.multiple_of(r * 32, 32), 32)
            sums[i, at, :] = jnp.zeros((32, NEV), jnp.float32)
            flips[i, at, :] = jnp.zeros((32, NEV), jnp.float32)

    rows_out[...] = jnp.zeros_like(rows_out)
    pair_copy.wait_recv()
    pair_load = pltpu.make_async_copy(pairs_in, pairs_other, load_sem)
    pair_load.start()
    pair_load.wait()

    @pl.when(core == 0)
    def _():
        @pl.loop(0, PIECES)
        def _(j):
            to_left(j).wait_recv()
            feed_ahead(j).start()

        @pl.loop(0, PIECES)
        def _(j):
            to_right(j).start()

    def pair(of_group, which, side):
        return jnp.where(of_group == group, pairs_own[which, side], pairs_other[which, side])

    def widen(n):
        at = pl.ds(pl.multiple_of(n * ROWS, ROWS), ROWS)
        for momentum in range(4):
            real = source[momentum // 2, momentum % 2, 0, at, :]
            imag = source[momentum // 2, momentum % 2, 1, at, :]
            wide[momentum, n, :ROWS, :NEV] = real
            wide[momentum, n, :ROWS, NEV:] = -imag
            wide[momentum, n, ROWS:, :NEV] = imag
            wide[momentum, n, ROWS:, NEV:] = real

    def work(slot, target, of_group, n):
        at = pl.ds(pl.multiple_of(n * ROWS, ROWS), ROWS)
        diagonal = (
            lax.broadcasted_iota(jnp.int32, (ROWS, NEV), 0) + n * ROWS
            == lax.broadcasted_iota(jnp.int32, (ROWS, NEV), 1)
        )
        for which in range(PAIRS):
            i = slot * PAIRS + which
            a = pair(of_group, which, 0)
            b = lax.rem(pair(of_group, which, 1), 2)
            full = jnp.dot(
                wide[a, n], target[b].reshape(2 * NEV, NEV), preferred_element_type=jnp.float32
            )
            real, imag = full[:ROWS], full[ROWS:]
            plus = real + imag
            flipped = (real - imag).T
            box = folded(plus * flips[i, at, :])
            sums[i, at, :] = plus
            flips[i, :, at] = flipped
            boxes[i] += box + folded(sums[i, :, at] * flipped)
            directs[i] += folded(jnp.where(diagonal, real, 0.0))

    @pl.loop(0, 3 * CHUNKS + 1)
    def _(step):
        for q in range(SUB):

            @pl.when(step < CHUNKS)
            def _():
                j = step * SUB + q
                to_right(j).wait_recv()
                over_y(j).start()

                @pl.when(core == 1)
                def _():
                    feed_source(j).start()

            if q == SUB - 1:

                @pl.when((step == CHUNKS - 1) & (core == 1))
                def _():
                    @pl.loop(0, PIECES)
                    def _(j):
                        to_left(j).start()

            first = (step >= 1) & (step <= CHUNKS)
            if q == 0:

                @pl.when(first)
                def _():
                    for piece in range(SUB):
                        over_y((step - 1) * SUB + piece).wait_recv()
                    widen(step - 1)
                    work(0, own, group, step - 1)

            if q == 1:

                @pl.when(step == 1)
                def _():
                    near_copy.wait_recv()

                @pl.when(first)
                def _():
                    work(1, near, group, step - 1)

            if q == 2:
                begin = 1 + core * CHUNKS

                @pl.when(step == begin)
                def _():
                    @pl.loop(0, PIECES)
                    def _(j):
                        feed_ahead(j).wait_recv()

                @pl.when((step >= begin) & (step < begin + CHUNKS))
                def _():
                    work(2, fed, jnp.where(core == 0, from_left, from_right), step - begin)

            if q == 3:
                begin = 1 + core * 2 * CHUNKS

                @pl.when((step == begin) & (core == 1))
                def _():
                    @pl.loop(0, PIECES)
                    def _(j):
                        to_left(j).wait_recv()

                @pl.when((step >= begin) & (step < begin + CHUNKS))
                def _():
                    work(3, ahead, from_right, step - begin)

    @pl.loop(0, PIECES)
    def _(j):
        to_right(j).wait_send()
        to_left(j).wait_send()
        over_y(j).wait_send()
        feed_ahead(j).wait_send()

    near_copy.wait_send()
    pair_copy.wait_send()

    separations = (1, 2 - 2 * core, 2 * core, 3)
    groups = (group, group, jnp.where(core == 0, from_left, from_right), from_right)
    for slot in range(SEPS):
        for kind, values in enumerate((directs, boxes)):
            for which in range(PAIRS):
                row = ((groups[slot] * 2 + kind) * SEPS + separations[slot]) * PAIRS + which
                rows_out[pl.ds(row, 1), :] = values[slot * PAIRS + which].sum(0, keepdims=True)
    lanes = jnp.broadcast_to(rows_out[...].sum(1, keepdims=True), (128, 128)).T
    tile[...] = lanes[:8]


def sum_kernel(
    tile, times, total, back, first, second, third, after_first, after_second,
    back_send, back_recv, send_1, recv_1, send_2, recv_2, send_3, recv_3,
):
    time, group = lax.axis_index("tm"), lax.axis_index("mom")
    count = lax.axis_size("tm")
    row, level, plane = time % 8, time // 8 % 8, time // 64
    before, behind = (time + count - 2) % count, (time + 2) % count
    in_row = [(row + d) % 8 for d in range(1, 8)]
    in_column = [(level + d) % 8 for d in range(1, 8)]
    corner = plane * 2 + group
    in_plane = [(corner + d) % 4 for d in range(1, 4)]
    row_devices = [{"tm": time - row + r, "mom": group} for r in in_row]
    column_devices = [{"tm": time + (r - level) * 8, "mom": group} for r in in_column]
    plane_devices = [{"tm": time + (r // 2 - plane) * 64, "mom": r % 2} for r in in_plane]
    back_devices = [{"tm": before, "mom": h} for h in range(2)]

    barrier = pltpu.get_barrier_semaphore()
    greeted = row_devices + column_devices + plane_devices + back_devices + [{"tm": behind, "mom": h} for h in range(2)]
    for device in greeted:
        pl.semaphore_signal(barrier, inc=1, device_id=device, device_id_type=MESH)
    pl.semaphore_wait(barrier, len(greeted))

    def remote(src, dst, send, recv, device):
        return pltpu.make_async_remote_copy(
            src_ref=src, dst_ref=dst, send_sem=send, recv_sem=recv, device_id=device, device_id_type=MESH
        )

    returns = [
        remote(tile, back.at[group], back_send.at[h], back_recv.at[group], device)
        for h, device in enumerate(back_devices)
    ]
    for copy in returns:
        copy.start()

    def stage(src, held, mine, places, devices, send, recv):
        copies = [
            remote(src, held.at[mine], send.at[d], recv.at[mine], device) for d, device in enumerate(devices)
        ]
        for copy in copies:
            copy.start()
        held[mine] = src[...]
        for d, place_of in enumerate(places):
            remote(src, held.at[place_of], send.at[d], recv.at[place_of], devices[d]).wait_recv()
        value = functools.reduce(jnp.add, [held[i] for i in range(held.shape[0])])
        return copies, value

    copies_1, value = stage(tile, first, row, in_row, row_devices, send_1, recv_1)
    after_first[...] = value
    copies_2, value = stage(after_first, second, level, in_column, column_devices, send_2, recv_2)
    after_second[...] = value
    copies_3, value = stage(after_second, third, corner, in_plane, plane_devices, send_3, recv_3)
    total[...] = value
    for h in range(2):
        remote(tile, back.at[h], back_send.at[h], back_recv.at[h], back_devices[h]).wait_recv()
    times[...] = back[0] + back[1]
    for copy in returns + copies_1 + copies_2 + copies_3:
        copy.wait_send()


def reorder(tile, group, deltas):
    values = tile[0, : 2 * 2 * SEPS * PAIRS].reshape(2, 2, SEPS, PAIRS)
    mine = jnp.where(group == 0, values[0], values[1])
    picker = deltas[:, None] == jnp.arange(SEPS, dtype=jnp.int32)[None, :]
    return jnp.sum(jnp.where(picker[None, :, :, None], mine[:, None], 0.0), axis=2)


def per_device(fields, mom_pairs, deltas):
    group = lax.axis_index("mom")
    field = (2, 2, NEV, NEV)
    dma = pltpu.SemaphoreType.DMA
    tile = pl.pallas_call(
        trace_kernel,
        out_shape=jax.ShapeDtypeStruct((8, 128), jnp.float32),
        in_specs=[
            pl.BlockSpec(memory_space=pltpu.SMEM),
            pl.BlockSpec(memory_space=pltpu.VMEM),
            pl.BlockSpec(memory_space=pl.ANY),
        ],
        out_specs=pl.BlockSpec(memory_space=pltpu.VMEM),
        scratch_shapes=[
            pltpu.VMEM(field, jnp.bfloat16),
            pltpu.VMEM(field, jnp.bfloat16),
            pltpu.VMEM(field, jnp.bfloat16),
            pltpu.VMEM(field, jnp.bfloat16),
            pltpu.VMEM((2, *field), jnp.bfloat16),
            pltpu.VMEM((4, CHUNKS, 2 * ROWS, 2 * NEV), jnp.bfloat16),
            pltpu.VMEM((SEPS * PAIRS, NEV, NEV), jnp.float32),
            pltpu.VMEM((SEPS * PAIRS, NEV, NEV), jnp.float32),
            pltpu.VMEM((SEPS * PAIRS, 8, 128), jnp.float32),
            pltpu.VMEM((SEPS * PAIRS, 8, 128), jnp.float32),
            pltpu.VMEM((128, 128), jnp.float32),
            pltpu.VMEM((PAIRS, 2), jnp.int32),
            pltpu.SMEM((PAIRS, 2), jnp.int32),
            dma,
            dma((2,)),
            dma((2,)),
        ]
        + [dma((PIECES,))] * 8,
        compiler_params=pltpu.CompilerParams(
            collective_id=0, has_side_effects=True, vmem_limit_bytes=62 * 1024 * 1024
        ),
        name="traces",
    )(mom_pairs, mom_pairs, fields.reshape(field))
    times, total = pl.pallas_call(
        sum_kernel,
        out_shape=[jax.ShapeDtypeStruct((8, 128), jnp.float32)] * 2,
        in_specs=[pl.BlockSpec(memory_space=pltpu.VMEM)],
        out_specs=[pl.BlockSpec(memory_space=pltpu.VMEM)] * 2,
        scratch_shapes=[
            pltpu.VMEM((2, 8, 128), jnp.float32),
            pltpu.VMEM((8, 8, 128), jnp.float32),
            pltpu.VMEM((8, 8, 128), jnp.float32),
            pltpu.VMEM((4, 8, 128), jnp.float32),
            pltpu.VMEM((8, 128), jnp.float32),
            pltpu.VMEM((8, 128), jnp.float32),
            dma((2,)),
            dma((2,)),
            dma((7,)),
            dma((8,)),
            dma((7,)),
            dma((8,)),
            dma((3,)),
            dma((4,)),
        ],
        compiler_params=pltpu.CompilerParams(collective_id=1, has_side_effects=True),
        name="sums",
    )(tile)
    return reorder(times, group, deltas)[None], reorder(total, group, deltas)


def solution(mesh):
    return jax.shard_map(
        per_device,
        mesh=mesh,
        in_specs=(P("tm", "mom", None, None, None), P("mom", None), P()),
        out_specs=(P("tm", None, None, "mom"), P(None, None, "mom")),
        check_vma=False,
    )
```

time: 277 us -> 106 us (0.38); the launches traced: 272 us -> 106 us
  Pallas kernels: 0 us -> 100 us
  other arithmetic: 51.2 us -> 1.69 us
  starting transfers between devices: 47.6 us -> 0 us
  local copies, waits for them, and re-layouts: 48.4 us -> 2.87 us
  matrix products: 33.8 us -> 0 us
  blocking collectives: 32.8 us -> 0 us
  waiting for transfers between devices: 29.9 us -> 0 us
  between operations: 28.1 us -> 0.66 us
    pallas_call x0 -> x2, Pallas kernels: none -> 100 us  [the longest x1 71.9 us: per_device(): pl.pallas_call(trace_kernel, out_shape=jax.ShapeDtypeStruct((8, 128), jnp...]
    ppermute x4 -> x0, starting transfers between devices: 41.9 us -> none  [from_behind(): return lax.ppermute(block, axis, route)]
    dot_general x12 -> x0, matrix products: 33.8 us -> none  [products(): jnp.einsum('xij,yjk->xyik', source, target, preferred_element_type=jnp.fl...]
    psum x4 -> x0, blocking collectives: 32.8 us -> none  [over_axes(): array = lax.psum(array, axis)]
    reduce_sum x13 -> x1, other arithmetic: 31.7 us -> 0.1 us  [reorder(): jnp.sum(jnp.where(picker[None, :, :, None], mine[:, None], 0.0), axis=2)]
    all_to_all x1 -> x0, waiting for transfers between devices: 29.9 us -> none  [sent_to_all(): return lax.all_to_all(copies, axis, split_axis=0, concat_axis=0, tiled=True)]
    sub x12 -> x0, local copies, waits for them, and re-layouts: 23.2 us -> none  [products(): real_part = product_full[0, 0] - product_full[1, 1]]
    add x12 -> x0, local copies, waits for them, and re-layouts: 17.3 us -> none  [products(): imag_part = product_full[0, 1] + product_full[1, 0]]
  transfers between devices with their start and end apart: 5 -> 0, of which waited for: 1 -> 0; matrix products, arithmetic and copies ran while one was open for 28% -> 0% of each run, Pallas kernels for 0% -> 0%
where the time goes in v1:
time: 106 us
  Pallas kernels  100 us (94%)
  local copies, waits for them, and re-layouts  2.87 us (3%)
  other arithmetic  1.69 us (2%)
    pallas_call x1, Pallas kernels, per_device(): pl.pallas_call(trace_kernel, out_shape=jax.ShapeDtypeStruct((8, 128), jnp...  71.9 us
    pallas_call x1, Pallas kernels, per_device(): pl.pallas_call(sum_kernel, out_shape=[jax.ShapeDtypeStruct((8, 128), jnp....  28.6 us

profile of v1, /device:TPU:1, one launch (start us, length us, event | category | flops | bytes accessed | tf_op | source)
XLA Modules:
  0.0 105.7 jit_solution(6205043302888443952)
XLA Ops:
  0.6 0.7 iota_compare_fusion
  1.4 1.3 %copy.9.pairs_own.pairs_sent = s32[3,2]{1,0:T(4,128)} copy(s32[3,2]{0,1:T(2,128)} %param.4) | data formatting | bytes 48 | tf_op args[1]
  2.7 71.9 %traces.1.tile = f32[8,128]{1,0:T(8,128)} custom-call(s32[3,2]{1,0:T(4,128)} %copy.9.pairs_own.pairs_sent, s32[3,2]{1,0:T(4,128)} %copy.9.pairs_own.pairs_sent, bf16[2,2,512,512]{3,2,1,0:T(8,128)(2,1)} %bitcast.4), custom_call_target="tpu_custom_call" | custom-call | tf_op jit(solution)/shard_map/traces/pallas_call | solution.py:327
  74.6 28.6 %sums.1 = (f32[8,128]{1,0:T(8,128)}, f32[8,128]{1,0:T(8,128)}) custom-call(f32[8,128]{1,0:T(8,128)} %traces.1.tile), custom_call_target="tpu_custom_call" | custom-call | tf_op jit(solution)/shard_map/sums/pallas_call | solution.py:360
  103.2 0.9 fusion
  104.1 0.1 select_n.35
  104.2 0.1 copy.11
  104.3 0.1 select_n.38
  104.3 0.1 copy.13
  104.4 0.1 select_reduce_fusion
  104.6 0.6 copy.14
  105.1 0.6 copy.16

commit v2 on v1

--- a/solution.py
+++ b/solution.py
@@ -39,9 +39,9 @@
 
 
 def trace_kernel(
-    pairs_own, pairs_sent, fields, tile,
+    pairs_own, pairs_sent, deltas, fields, tile,
     own, near, fed, ahead, source, wide, sums, flips, boxes, directs, rows_out, pairs_in, pairs_other,
-    load_sem, pair_sems, near_sems, send_right, recv_right, send_left, recv_left, send_y, recv_y, send_core, recv_core,
+    ready, load_sem, pair_sems, near_sems, send_right, recv_right, send_left, recv_left, send_y, recv_y, send_core, recv_core,
 ):
     time, group, core, right, left, across, partner = place()
     from_left = left["mom"]
@@ -55,13 +55,13 @@
             src_ref=src, dst_ref=dst, send_sem=send, recv_sem=recv, device_id=device, device_id_type=MESH
         )
 
-    def to_right(j):
+    def to_right(j, held=own):
         return remote(
-            own.at[:, :, rows(j), :], source.at[group, :, :, rows(j), :], send_right.at[j], recv_right.at[j], right
+            held.at[:, :, rows(j), :], source.at[group, :, :, rows(j), :], send_right.at[j], recv_right.at[j], right
         )
 
-    def to_left(j):
-        return remote(own.at[:, :, rows(j), :], ahead.at[:, :, rows(j), :], send_left.at[j], recv_left.at[j], left)
+    def to_left(j, held=own):
+        return remote(held.at[:, :, rows(j), :], ahead.at[:, :, rows(j), :], send_left.at[j], recv_left.at[j], left)
 
     def over_y(j):
         part = source.at[from_left, :, :, rows(j), :]
@@ -75,28 +75,30 @@
     def feed_ahead(j):
         return remote(ahead.at[:, :, rows(j), :], fed.at[:, :, rows(j), :], send_core.at[j], recv_core.at[j], partner)
 
-    near_copy = remote(own, near, near_sems.at[0], near_sems.at[1], partner)
+    near_copy = remote(fields, near, near_sems.at[0], near_sems.at[1], partner)
     pair_copy = remote(pairs_sent, pairs_in, pair_sems.at[0], pair_sems.at[1], across)
     load = pltpu.make_async_copy(fields, own, load_sem)
 
     barrier = pltpu.get_barrier_semaphore()
+    for device in (left, across, partner):
+        pl.semaphore_signal(barrier, inc=1, device_id=device, device_id_type=MESH)
     load.start()
-    for device in (right, left, across, partner):
-        pl.semaphore_signal(barrier, inc=1, device_id=device, device_id_type=MESH)
-    load.wait()
-    pl.semaphore_wait(barrier, 4)
+    pl.semaphore_wait(barrier, 3)
+    pl.semaphore_signal(ready, inc=1, device_id=right, device_id_type=MESH)
 
     @pl.when(core == 1)
     def _():
         @pl.loop(0, PIECES)
         def _(j):
-            to_right(j).start()
+            to_right(j, fields).start()
 
     @pl.when(core == 0)
     def _():
+        pl.semaphore_wait(ready, 1)
+
         @pl.loop(0, PIECES)
         def _(j):
-            to_left(j).start()
+            to_left(j, fields).start()
 
     pair_copy.start()
     near_copy.start()
@@ -113,6 +115,7 @@
             flips[i, at, :] = jnp.zeros((32, NEV), jnp.float32)
 
     rows_out[...] = jnp.zeros_like(rows_out)
+    load.wait()
     pair_copy.wait_recv()
     pair_load = pltpu.make_async_copy(pairs_in, pairs_other, load_sem)
     pair_load.start()
@@ -125,12 +128,14 @@
             to_left(j).wait_recv()
             feed_ahead(j).start()
 
-        @pl.loop(0, PIECES)
-        def _(j):
-            to_right(j).start()
+            @pl.when(j == PIECES - 3)
+            def _():
+                @pl.loop(0, PIECES)
+                def _(k):
+                    to_right(k).start()
 
     def pair(of_group, which, side):
-        return jnp.where(of_group == group, pairs_own[which, side], pairs_other[which, side])
+        return jnp.where(of_group == group, pairs_own[side, which], pairs_other[side, which])
 
     def widen(n):
         at = pl.ds(pl.multiple_of(n * ROWS, ROWS), ROWS)
@@ -164,6 +169,10 @@
             boxes[i] += box + folded(sums[i, :, at] * flipped)
             directs[i] += folded(jnp.where(diagonal, real, 0.0))
 
+    fed_group = jnp.where(core == 0, from_left, from_right)
+    fed_step = 2 + 3 * core
+    ahead_step = 2 + (3 + CHUNKS) * core
+
     @pl.loop(0, 3 * CHUNKS + 1)
     def _(step):
         for q in range(SUB):
@@ -178,59 +187,56 @@
                 def _():
                     feed_source(j).start()
 
-            if q == SUB - 1:
+            if q == 0:
+
+                @pl.when(step == fed_step)
+                def _():
+                    @pl.loop(0, PIECES)
+                    def _(j):
+                        feed_ahead(j).wait_recv()
+
+                @pl.when((step >= fed_step) & (step < fed_step + CHUNKS))
+                def _():
+                    work(2, fed, fed_group, step - fed_step)
+
+            if q == 1:
 
                 @pl.when((step == CHUNKS - 1) & (core == 1))
                 def _():
+                    pl.semaphore_wait(ready, 1)
+
                     @pl.loop(0, PIECES)
                     def _(j):
                         to_left(j).start()
 
-            first = (step >= 1) & (step <= CHUNKS)
-            if q == 0:
-
-                @pl.when(first)
+                @pl.when((step == ahead_step) & (core == 1))
+                def _():
+                    @pl.loop(0, PIECES)
+                    def _(j):
+                        to_left(j).wait_recv()
+
+                @pl.when((step >= ahead_step) & (step < ahead_step + CHUNKS))
+                def _():
+                    work(3, ahead, from_right, step - ahead_step)
+
+            if q == 2:
+
+                @pl.when((step >= 1) & (step <= CHUNKS))
                 def _():
                     for piece in range(SUB):
                         over_y((step - 1) * SUB + piece).wait_recv()
                     widen(step - 1)
                     work(0, own, group, step - 1)
 
-            if q == 1:
+            if q == 3:
 
                 @pl.when(step == 1)
                 def _():
                     near_copy.wait_recv()
 
-                @pl.when(first)
+                @pl.when((step >= 1) & (step <= CHUNKS))
                 def _():
                     work(1, near, group, step - 1)
-
-            if q == 2:
-                begin = 1 + core * CHUNKS
-
-                @pl.when(step == begin)
-                def _():
-                    @pl.loop(0, PIECES)
-                    def _(j):
-                        feed_ahead(j).wait_recv()
-
-                @pl.when((step >= begin) & (step < begin + CHUNKS))
-                def _():
-                    work(2, fed, jnp.where(core == 0, from_left, from_right), step - begin)
-
-            if q == 3:
-                begin = 1 + core * 2 * CHUNKS
-
-                @pl.when((step == begin) & (core == 1))
-                def _():
-                    @pl.loop(0, PIECES)
-                    def _(j):
-                        to_left(j).wait_recv()
-
-                @pl.when((step >= begin) & (step < begin + CHUNKS))
-                def _():
-                    work(3, ahead, from_right, step - begin)
 
     @pl.loop(0, PIECES)
     def _(j):
@@ -243,14 +249,32 @@
     pair_copy.wait_send()
 
     separations = (1, 2 - 2 * core, 2 * core, 3)
-    groups = (group, group, jnp.where(core == 0, from_left, from_right), from_right)
+    groups = (group, group, fed_group, from_right)
+    lane = lax.broadcasted_iota(jnp.int32, (8, 128), 1)
+    wanted = functools.reduce(
+        jnp.add, [jnp.where(lane % SEPS == r, deltas[r], 0) for r in range(SEPS)]
+    )
     for slot in range(SEPS):
         for kind, values in enumerate((directs, boxes)):
             for which in range(PAIRS):
-                row = ((groups[slot] * 2 + kind) * SEPS + separations[slot]) * PAIRS + which
-                rows_out[pl.ds(row, 1), :] = values[slot * PAIRS + which].sum(0, keepdims=True)
-    lanes = jnp.broadcast_to(rows_out[...].sum(1, keepdims=True), (128, 128)).T
-    tile[...] = lanes[:8]
+                row = slot * 8 + which * 2 + kind
+                rows_out[row : row + 1, :] = values[slot * PAIRS + which].sum(0, keepdims=True)
+    totals = jnp.broadcast_to(rows_out[...].sum(1, keepdims=True), rows_out.shape)
+    tile[...] = functools.reduce(
+        jnp.add,
+        [
+            jnp.where(
+                (wanted == separations[slot]) & (lane // SEPS == groups[slot]), totals[slot * 8 : slot * 8 + 8], 0.0
+            )
+            for slot in range(SEPS)
+        ],
+    )
+
+
+def deliver(values, out, group):
+    mine = jnp.where(group == 0, values[:, :SEPS], values[:, SEPS : 2 * SEPS])
+    for which in range(PAIRS):
+        out[which] = mine[which * 2 : which * 2 + 2]
 
 
 def sum_kernel(
@@ -305,23 +329,15 @@
     copies_2, value = stage(after_first, second, level, in_column, column_devices, send_2, recv_2)
     after_second[...] = value
     copies_3, value = stage(after_second, third, corner, in_plane, plane_devices, send_3, recv_3)
-    total[...] = value
+    deliver(value, total, group)
     for h in range(2):
         remote(tile, back.at[h], back_send.at[h], back_recv.at[h], back_devices[h]).wait_recv()
-    times[...] = back[0] + back[1]
+    deliver(back[0] + back[1], times, group)
     for copy in returns + copies_1 + copies_2 + copies_3:
         copy.wait_send()
 
 
-def reorder(tile, group, deltas):
-    values = tile[0, : 2 * 2 * SEPS * PAIRS].reshape(2, 2, SEPS, PAIRS)
-    mine = jnp.where(group == 0, values[0], values[1])
-    picker = deltas[:, None] == jnp.arange(SEPS, dtype=jnp.int32)[None, :]
-    return jnp.sum(jnp.where(picker[None, :, :, None], mine[:, None], 0.0), axis=2)
-
-
 def per_device(fields, mom_pairs, deltas):
-    group = lax.axis_index("mom")
     field = (2, 2, NEV, NEV)
     dma = pltpu.SemaphoreType.DMA
     tile = pl.pallas_call(
@@ -330,6 +346,7 @@
         in_specs=[
             pl.BlockSpec(memory_space=pltpu.SMEM),
             pl.BlockSpec(memory_space=pltpu.VMEM),
+            pl.BlockSpec(memory_space=pltpu.SMEM),
             pl.BlockSpec(memory_space=pl.ANY),
         ],
         out_specs=pl.BlockSpec(memory_space=pltpu.VMEM),
@@ -344,9 +361,10 @@
             pltpu.VMEM((SEPS * PAIRS, NEV, NEV), jnp.float32),
             pltpu.VMEM((SEPS * PAIRS, 8, 128), jnp.float32),
             pltpu.VMEM((SEPS * PAIRS, 8, 128), jnp.float32),
-            pltpu.VMEM((128, 128), jnp.float32),
-            pltpu.VMEM((PAIRS, 2), jnp.int32),
-            pltpu.SMEM((PAIRS, 2), jnp.int32),
+            pltpu.VMEM((SEPS * 8, 128), jnp.float32),
+            pltpu.VMEM((2, PAIRS), jnp.int32),
+            pltpu.SMEM((2, PAIRS), jnp.int32),
+            pltpu.SemaphoreType.REGULAR,
             dma,
             dma((2,)),
             dma((2,)),
@@ -356,10 +374,10 @@
             collective_id=0, has_side_effects=True, vmem_limit_bytes=62 * 1024 * 1024
         ),
         name="traces",
-    )(mom_pairs, mom_pairs, fields.reshape(field))
+    )(mom_pairs.T, mom_pairs.T, deltas, fields.reshape(field))
     times, total = pl.pallas_call(
         sum_kernel,
-        out_shape=[jax.ShapeDtypeStruct((8, 128), jnp.float32)] * 2,
+        out_shape=[jax.ShapeDtypeStruct((PAIRS, 2, SEPS), jnp.float32)] * 2,
         in_specs=[pl.BlockSpec(memory_space=pltpu.VMEM)],
         out_specs=[pl.BlockSpec(memory_space=pltpu.VMEM)] * 2,
         scratch_shapes=[
@@ -381,7 +399,7 @@
         compiler_params=pltpu.CompilerParams(collective_id=1, has_side_effects=True),
         name="sums",
     )(tile)
-    return reorder(times, group, deltas)[None], reorder(total, group, deltas)
+    return times.transpose(1, 2, 0)[None], total.transpose(1, 2, 0)
 
 
 def solution(mesh):

time: 106 us -> 95.5 us (0.901)
  Pallas kernels: 100 us -> 92 us
  other arithmetic: 1.69 us -> 0 us
    pallas_call x1, Pallas kernels: 71.9 us -> 61.5 us  [per_device(): pl.pallas_call(trace_kernel, out_shape=jax.ShapeDtypeStruct((8, 128), jnp...]
    pallas_call x1, Pallas kernels: 28.6 us -> 30.5 us  [per_device(): pl.pallas_call(sum_kernel, out_shape=[jax.ShapeDtypeStruct((PAIRS, 2, SEP...]
where the time goes in v2:
time: 95.5 us; the launch traced here: 95.1 us
  Pallas kernels  92 us (96%)
  local copies, waits for them, and re-layouts  2.49 us (3%)
    pallas_call x1, Pallas kernels, per_device(): pl.pallas_call(trace_kernel, out_shape=jax.ShapeDtypeStruct((8, 128), jnp...  61.5 us
    pallas_call x1, Pallas kernels, per_device(): pl.pallas_call(sum_kernel, out_shape=[jax.ShapeDtypeStruct((PAIRS, 2, SEP...  30.5 us
    unnamed x2, local copies, waits for them, and re-layouts  2.49 us

profile of v2, /device:TPU:1, one launch (start us, length us, event | category | flops | bytes accessed | tf_op | source)
XLA Modules:
  0.0 95.1 jit_solution(13460270026338447001)
XLA Ops:
  0.6 61.5 %traces.1.tile = f32[8,128]{1,0:T(8,128)} custom-call(s32[2,3]{1,0:T(2,128)} %bitcast.7, s32[2,3]{1,0:T(2,128)} %bitcast.8, s32[4]{0:T(128)} %deltas.1, bf16[2,2,512,512]{3,2,1,0:T(8,128)(2,1)} %bitcast.6), custom_call_target="tpu_custom_call" | custom-call | tf_op jit(solution)/shard_map/traces/pallas_call | solution.py:343
  62.1 30.5 %sums.1 = (f32[3,2,4]{2,1,0:T(2,128)}, f32[3,2,4]{2,1,0:T(2,128)}) custom-call(f32[8,128]{1,0:T(8,128)} %traces.1.tile), custom_call_target="tpu_custom_call" | custom-call | tf_op jit(solution)/shard_map/sums/pallas_call | solution.py:378
  92.6 1.2 %copy.7 = f32[1,2,4,3]{2,1,3,0:T(2,128)} copy(f32[1,2,4,3]{2,1,3,0:T(2,128)} %bitcast.10) | data formatting | bytes 192
  93.8 1.3 %copy.8 = f32[2,4,3]{1,0,2:T(2,128)} copy(f32[2,4,3]{1,0,2:T(2,128)} %bitcast.9) | data formatting | bytes 192

commit v3 on v2

--- a/solution.py
+++ b/solution.py
@@ -39,9 +39,10 @@
 
 
 def trace_kernel(
-    pairs_own, pairs_sent, deltas, fields, tile,
+    pairs_own, pairs_sent, deltas, fields, results,
     own, near, fed, ahead, source, wide, sums, flips, boxes, directs, rows_out, pairs_in, pairs_other,
-    ready, load_sem, pair_sems, near_sems, send_right, recv_right, send_left, recv_left, send_y, recv_y, send_core, recv_core,
+    tile, back, first, second, third, after_first, after_second, load_sem, pair_sems, near_sems, send_right, recv_right, send_left, recv_left, send_y, recv_y, send_core, recv_core,
+    back_send, back_recv, send_1, recv_1, send_2, recv_2, send_3, recv_3,
 ):
     time, group, core, right, left, across, partner = place()
     from_left = left["mom"]
@@ -79,12 +80,24 @@
     pair_copy = remote(pairs_sent, pairs_in, pair_sems.at[0], pair_sems.at[1], across)
     load = pltpu.make_async_copy(fields, own, load_sem)
 
+    count = lax.axis_size("tm")
+    row, level, plane = time % 8, time // 8 % 8, time // 64
+    in_row = [(row + d) % 8 for d in range(1, 8)]
+    in_column = [(level + d) % 8 for d in range(1, 8)]
+    corner = plane * 2 + group
+    in_plane = [(corner + d) % 4 for d in range(1, 4)]
+    row_devices = [{"tm": time - row + r, "mom": group} for r in in_row]
+    column_devices = [{"tm": time + (r - level) * 8, "mom": group} for r in in_column]
+    plane_devices = [{"tm": time + (r // 2 - plane) * 64, "mom": r % 2} for r in in_plane]
+    back_devices = [{"tm": (time + count - 2) % count, "mom": h} for h in range(2)]
+    behind_devices = [{"tm": (time + 2) % count, "mom": h} for h in range(2)]
+
     barrier = pltpu.get_barrier_semaphore()
-    for device in (left, across, partner):
+    greeted = column_devices + plane_devices + row_devices + back_devices + behind_devices
+    for device in greeted:
         pl.semaphore_signal(barrier, inc=1, device_id=device, device_id_type=MESH)
     load.start()
-    pl.semaphore_wait(barrier, 3)
-    pl.semaphore_signal(ready, inc=1, device_id=right, device_id_type=MESH)
+    pl.semaphore_wait(barrier, len(greeted))
 
     @pl.when(core == 1)
     def _():
@@ -94,8 +107,6 @@
 
     @pl.when(core == 0)
     def _():
-        pl.semaphore_wait(ready, 1)
-
         @pl.loop(0, PIECES)
         def _(j):
             to_left(j, fields).start()
@@ -201,25 +212,23 @@
 
             if q == 1:
 
+                @pl.when((step == ahead_step) & (core == 1))
+                def _():
+                    @pl.loop(0, PIECES)
+                    def _(j):
+                        to_left(j).wait_recv()
+
+                @pl.when((step >= ahead_step) & (step < ahead_step + CHUNKS))
+                def _():
+                    work(3, ahead, from_right, step - ahead_step)
+
+            if q == 2:
+
                 @pl.when((step == CHUNKS - 1) & (core == 1))
                 def _():
-                    pl.semaphore_wait(ready, 1)
-
                     @pl.loop(0, PIECES)
                     def _(j):
                         to_left(j).start()
-
-                @pl.when((step == ahead_step) & (core == 1))
-                def _():
-                    @pl.loop(0, PIECES)
-                    def _(j):
-                        to_left(j).wait_recv()
-
-                @pl.when((step >= ahead_step) & (step < ahead_step + CHUNKS))
-                def _():
-                    work(3, ahead, from_right, step - ahead_step)
-
-            if q == 2:
 
                 @pl.when((step >= 1) & (step <= CHUNKS))
                 def _():
@@ -237,16 +246,6 @@
                 @pl.when((step >= 1) & (step <= CHUNKS))
                 def _():
                     work(1, near, group, step - 1)
-
-    @pl.loop(0, PIECES)
-    def _(j):
-        to_right(j).wait_send()
-        to_left(j).wait_send()
-        over_y(j).wait_send()
-        feed_ahead(j).wait_send()
-
-    near_copy.wait_send()
-    pair_copy.wait_send()
 
     separations = (1, 2 - 2 * core, 2 * core, 3)
     groups = (group, group, fed_group, from_right)
@@ -257,8 +256,8 @@
     for slot in range(SEPS):
         for kind, values in enumerate((directs, boxes)):
             for which in range(PAIRS):
-                row = slot * 8 + which * 2 + kind
-                rows_out[row : row + 1, :] = values[slot * PAIRS + which].sum(0, keepdims=True)
+                line = slot * 8 + which * 2 + kind
+                rows_out[line : line + 1, :] = values[slot * PAIRS + which].sum(0, keepdims=True)
     totals = jnp.broadcast_to(rows_out[...].sum(1, keepdims=True), rows_out.shape)
     tile[...] = functools.reduce(
         jnp.add,
@@ -270,41 +269,6 @@
         ],
     )
 
-
-def deliver(values, out, group):
-    mine = jnp.where(group == 0, values[:, :SEPS], values[:, SEPS : 2 * SEPS])
-    for which in range(PAIRS):
-        out[which] = mine[which * 2 : which * 2 + 2]
-
-
-def sum_kernel(
-    tile, times, total, back, first, second, third, after_first, after_second,
-    back_send, back_recv, send_1, recv_1, send_2, recv_2, send_3, recv_3,
-):
-    time, group = lax.axis_index("tm"), lax.axis_index("mom")
-    count = lax.axis_size("tm")
-    row, level, plane = time % 8, time // 8 % 8, time // 64
-    before, behind = (time + count - 2) % count, (time + 2) % count
-    in_row = [(row + d) % 8 for d in range(1, 8)]
-    in_column = [(level + d) % 8 for d in range(1, 8)]
-    corner = plane * 2 + group
-    in_plane = [(corner + d) % 4 for d in range(1, 4)]
-    row_devices = [{"tm": time - row + r, "mom": group} for r in in_row]
-    column_devices = [{"tm": time + (r - level) * 8, "mom": group} for r in in_column]
-    plane_devices = [{"tm": time + (r // 2 - plane) * 64, "mom": r % 2} for r in in_plane]
-    back_devices = [{"tm": before, "mom": h} for h in range(2)]
-
-    barrier = pltpu.get_barrier_semaphore()
-    greeted = row_devices + column_devices + plane_devices + back_devices + [{"tm": behind, "mom": h} for h in range(2)]
-    for device in greeted:
-        pl.semaphore_signal(barrier, inc=1, device_id=device, device_id_type=MESH)
-    pl.semaphore_wait(barrier, len(greeted))
-
-    def remote(src, dst, send, recv, device):
-        return pltpu.make_async_remote_copy(
-            src_ref=src, dst_ref=dst, send_sem=send, recv_sem=recv, device_id=device, device_id_type=MESH
-        )
-
     returns = [
         remote(tile, back.at[group], back_send.at[h], back_recv.at[group], device)
         for h, device in enumerate(back_devices)
@@ -321,28 +285,42 @@
         held[mine] = src[...]
         for d, place_of in enumerate(places):
             remote(src, held.at[place_of], send.at[d], recv.at[place_of], devices[d]).wait_recv()
-        value = functools.reduce(jnp.add, [held[i] for i in range(held.shape[0])])
-        return copies, value
+        return copies, functools.reduce(jnp.add, [held[i] for i in range(held.shape[0])])
+
+    def deliver(values, out):
+        mine = jnp.where(group == 0, values[:, :SEPS], values[:, SEPS : 2 * SEPS])
+        for which in range(PAIRS):
+            results[out, which] = mine[which * 2 : which * 2 + 2]
 
     copies_1, value = stage(tile, first, row, in_row, row_devices, send_1, recv_1)
     after_first[...] = value
     copies_2, value = stage(after_first, second, level, in_column, column_devices, send_2, recv_2)
     after_second[...] = value
     copies_3, value = stage(after_second, third, corner, in_plane, plane_devices, send_3, recv_3)
-    deliver(value, total, group)
+    deliver(value, 1)
     for h in range(2):
         remote(tile, back.at[h], back_send.at[h], back_recv.at[h], back_devices[h]).wait_recv()
-    deliver(back[0] + back[1], times, group)
+    deliver(back[0] + back[1], 0)
     for copy in returns + copies_1 + copies_2 + copies_3:
         copy.wait_send()
+
+    @pl.loop(0, PIECES)
+    def _(j):
+        to_right(j).wait_send()
+        to_left(j).wait_send()
+        over_y(j).wait_send()
+        feed_ahead(j).wait_send()
+
+    near_copy.wait_send()
+    pair_copy.wait_send()
 
 
 def per_device(fields, mom_pairs, deltas):
     field = (2, 2, NEV, NEV)
     dma = pltpu.SemaphoreType.DMA
-    tile = pl.pallas_call(
+    results = pl.pallas_call(
         trace_kernel,
-        out_shape=jax.ShapeDtypeStruct((8, 128), jnp.float32),
+        out_shape=jax.ShapeDtypeStruct((2, PAIRS, 2, SEPS), jnp.float32),
         in_specs=[
             pl.BlockSpec(memory_space=pltpu.SMEM),
             pl.BlockSpec(memory_space=pltpu.VMEM),
@@ -364,42 +342,26 @@
             pltpu.VMEM((SEPS * 8, 128), jnp.float32),
             pltpu.VMEM((2, PAIRS), jnp.int32),
             pltpu.SMEM((2, PAIRS), jnp.int32),
-            pltpu.SemaphoreType.REGULAR,
-            dma,
-            dma((2,)),
-            dma((2,)),
-        ]
-        + [dma((PIECES,))] * 8,
-        compiler_params=pltpu.CompilerParams(
-            collective_id=0, has_side_effects=True, vmem_limit_bytes=62 * 1024 * 1024
-        ),
-        name="traces",
-    )(mom_pairs.T, mom_pairs.T, deltas, fields.reshape(field))
-    times, total = pl.pallas_call(
-        sum_kernel,
-        out_shape=[jax.ShapeDtypeStruct((PAIRS, 2, SEPS), jnp.float32)] * 2,
-        in_specs=[pl.BlockSpec(memory_space=pltpu.VMEM)],
-        out_specs=[pl.BlockSpec(memory_space=pltpu.VMEM)] * 2,
-        scratch_shapes=[
+            pltpu.VMEM((8, 128), jnp.float32),
             pltpu.VMEM((2, 8, 128), jnp.float32),
             pltpu.VMEM((8, 8, 128), jnp.float32),
             pltpu.VMEM((8, 8, 128), jnp.float32),
             pltpu.VMEM((4, 8, 128), jnp.float32),
             pltpu.VMEM((8, 128), jnp.float32),
             pltpu.VMEM((8, 128), jnp.float32),
+            dma,
             dma((2,)),
             dma((2,)),
-            dma((7,)),
-            dma((8,)),
-            dma((7,)),
-            dma((8,)),
-            dma((3,)),
-            dma((4,)),
-        ],
-        compiler_params=pltpu.CompilerParams(collective_id=1, has_side_effects=True),
-        name="sums",
-    )(tile)
-    return times.transpose(1, 2, 0)[None], total.transpose(1, 2, 0)
+        ]
+        + [dma((PIECES,))] * 8
+        + [dma((n,)) for n in (2, 2, 7, 8, 7, 8, 3, 4)],
+        compiler_params=pltpu.CompilerParams(
+            collective_id=0, has_side_effects=True, vmem_limit_bytes=62 * 1024 * 1024
+        ),
+        name="traces",
+    )(mom_pairs.T, mom_pairs.T, deltas, fields.reshape(field))
+    times, total = results.transpose(0, 2, 3, 1)
+    return times[None], total
 
 
 def solution(mesh):

time: 95.5 us -> 85.9 us (0.90); the launches traced: 95.1 us -> 84.5 us
  Pallas kernels: 92 us -> 82.6 us
  local copies, waits for them, and re-layouts: 2.49 us -> 1.26 us
    pallas_call x2 -> x1, Pallas kernels: 92 us -> 82.6 us  [per_device(): pl.pallas_call(trace_kernel, out_shape=jax.ShapeDtypeStruct((2, PAIRS, 2,...]
    unnamed x2 -> x0, local copies, waits for them, and re-layouts: 2.49 us -> none
    another operation x0 -> x1, local copies, waits for them, and re-layouts: none -> 1.26 us  [per_device(): times, total = results.transpose(0, 2, 3, 1)]
where the time goes in v3:
time: 85.9 us; the launch traced here: 84.5 us
  Pallas kernels  82.6 us (96%)
  local copies, waits for them, and re-layouts  1.26 us (1%)
    pallas_call x1, Pallas kernels, per_device(): pl.pallas_call(trace_kernel, out_shape=jax.ShapeDtypeStruct((2, PAIRS, 2,...  82.6 us

profile of v3, /device:TPU:1, one launch (start us, length us, event | category | flops | bytes accessed | tf_op | source)
XLA Modules:
  0.0 84.5 jit_solution(17120839877194742233)
XLA Ops:
  0.6 82.6 %traces.1 = f32[2,3,2,4]{3,2,1,0:T(2,128)} custom-call(s32[2,3]{1,0:T(2,128)} %bitcast.7, s32[2,3]{1,0:T(2,128)} %bitcast.8, s32[4]{0:T(128)} %deltas.1, bf16[2,2,512,512]{3,2,1,0:T(8,128)(2,1)} %bitcast.5), custom_call_target="tpu_custom_call" | custom-call | tf_op jit(solution)/shard_map/traces/pallas_call | solution.py:321
  83.2 1.3 %slice_bitcast_fusion = (f32[2,4,3]{1,0,2:T(2,128)}, f32[1,2,4,3]{2,1,3,0:T(2,128)}) fusion(f32[2,2,4,3]{2,1,3,0:T(2,128)} %bitcast.6), kind=kLoop, calls=%fused_computation | loop fusion | bytes 384 | tf_op jit(solution)/shard_map/unstack | solution.py:363

commit v4 on v3

--- a/solution.py
+++ b/solution.py
@@ -39,12 +39,14 @@
 
 
 def trace_kernel(
-    pairs_own, pairs_sent, deltas, fields, results,
-    own, near, fed, ahead, source, wide, sums, flips, boxes, directs, rows_out, pairs_in, pairs_other,
+    pairs, deltas_in, fields, results,
+    own, near, fed, ahead, relay, source, wide, sums, flips, boxes, directs, rows_out, pairs_in, pairs_own, pairs_other, deltas,
     tile, back, first, second, third, after_first, after_second, load_sem, pair_sems, near_sems, send_right, recv_right, send_left, recv_left, send_y, recv_y, send_core, recv_core,
+    recv_relay, relay_sent_y, relay_sent_core,
     back_send, back_recv, send_1, recv_1, send_2, recv_2, send_3, recv_3,
 ):
     time, group, core, right, left, across, partner = place()
+    count = lax.axis_size("tm")
     from_left = left["mom"]
     from_right = right["mom"]
 
@@ -64,6 +66,21 @@
     def to_left(j, held=own):
         return remote(held.at[:, :, rows(j), :], ahead.at[:, :, rows(j), :], send_left.at[j], recv_left.at[j], left)
 
+    def to_relay(j):
+        device = {"tm": (time + 3) % count, "mom": right["mom"]}
+        return remote(
+            own.at[:, :, rows(j), :], relay.at[:, :, rows(j), :], send_right.at[j], recv_relay.at[j], device
+        )
+
+    def relay_y(j):
+        part = source.at[from_left, :, :, rows(j), :]
+        device = {"tm": partner["tm"], "mom": 1 - group}
+        return remote(relay.at[:, :, rows(j), :], part, relay_sent_y.at[j], recv_y.at[j], device)
+
+    def relay_core(j):
+        part = source.at[from_left, :, :, rows(j), :]
+        return remote(relay.at[:, :, rows(j), :], part, relay_sent_core.at[j], recv_right.at[j], partner)
+
     def over_y(j):
         part = source.at[from_left, :, :, rows(j), :]
         return remote(part, part, send_y.at[j], recv_y.at[j], across)
@@ -77,10 +94,9 @@
         return remote(ahead.at[:, :, rows(j), :], fed.at[:, :, rows(j), :], send_core.at[j], recv_core.at[j], partner)
 
     near_copy = remote(fields, near, near_sems.at[0], near_sems.at[1], partner)
-    pair_copy = remote(pairs_sent, pairs_in, pair_sems.at[0], pair_sems.at[1], across)
+    pair_copy = remote(pairs, pairs_in, pair_sems.at[0], pair_sems.at[1], across)
     load = pltpu.make_async_copy(fields, own, load_sem)
 
-    count = lax.axis_size("tm")
     row, level, plane = time % 8, time // 8 % 8, time // 64
     in_row = [(row + d) % 8 for d in range(1, 8)]
     in_column = [(level + d) % 8 for d in range(1, 8)]
@@ -93,10 +109,20 @@
     behind_devices = [{"tm": (time + 2) % count, "mom": h} for h in range(2)]
 
     barrier = pltpu.get_barrier_semaphore()
-    greeted = column_devices + plane_devices + row_devices + back_devices + behind_devices
+    relays = [
+        {"tm": partner["tm"], "mom": 1 - group},
+        {"tm": (time + count + 3 - 6 * core) % count, "mom": jnp.where(core == 0, right["mom"], left["mom"])},
+    ]
+    greeted = column_devices + plane_devices + row_devices + back_devices + behind_devices + relays
     for device in greeted:
         pl.semaphore_signal(barrier, inc=1, device_id=device, device_id_type=MESH)
+    own_tables = [
+        pltpu.make_async_copy(pairs, pairs_own, pair_sems.at[2]),
+        pltpu.make_async_copy(deltas_in, deltas, pair_sems.at[3]),
+    ]
     load.start()
+    for copy in own_tables:
+        copy.start()
     pl.semaphore_wait(barrier, len(greeted))
 
     @pl.when(core == 1)
@@ -127,23 +153,12 @@
 
     rows_out[...] = jnp.zeros_like(rows_out)
     load.wait()
+    for copy in own_tables:
+        copy.wait()
     pair_copy.wait_recv()
     pair_load = pltpu.make_async_copy(pairs_in, pairs_other, load_sem)
     pair_load.start()
     pair_load.wait()
-
-    @pl.when(core == 0)
-    def _():
-        @pl.loop(0, PIECES)
-        def _(j):
-            to_left(j).wait_recv()
-            feed_ahead(j).start()
-
-            @pl.when(j == PIECES - 3)
-            def _():
-                @pl.loop(0, PIECES)
-                def _(k):
-                    to_right(k).start()
 
     def pair(of_group, which, side):
         return jnp.where(of_group == group, pairs_own[side, which], pairs_other[side, which])
@@ -158,94 +173,133 @@
             wide[momentum, n, ROWS:, :NEV] = imag
             wide[momentum, n, ROWS:, NEV:] = real
 
-    def work(slot, target, of_group, n):
+    def work(targets, n):
         at = pl.ds(pl.multiple_of(n * ROWS, ROWS), ROWS)
         diagonal = (
             lax.broadcasted_iota(jnp.int32, (ROWS, NEV), 0) + n * ROWS
             == lax.broadcasted_iota(jnp.int32, (ROWS, NEV), 1)
         )
-        for which in range(PAIRS):
-            i = slot * PAIRS + which
-            a = pair(of_group, which, 0)
-            b = lax.rem(pair(of_group, which, 1), 2)
-            full = jnp.dot(
-                wide[a, n], target[b].reshape(2 * NEV, NEV), preferred_element_type=jnp.float32
-            )
-            real, imag = full[:ROWS], full[ROWS:]
-            plus = real + imag
-            flipped = (real - imag).T
-            box = folded(plus * flips[i, at, :])
-            sums[i, at, :] = plus
-            flips[i, :, at] = flipped
-            boxes[i] += box + folded(sums[i, :, at] * flipped)
-            directs[i] += folded(jnp.where(diagonal, real, 0.0))
+        for slot, target, of_group in targets:
+            for which in range(PAIRS):
+                i = slot * PAIRS + which
+                a = pair(of_group, which, 0)
+                b = lax.rem(pair(of_group, which, 1), 2)
+                full = jnp.dot(
+                    wide[a, n], target[b].reshape(2 * NEV, NEV), preferred_element_type=jnp.float32
+                )
+                real, imag = full[:ROWS], full[ROWS:]
+                plus = real + imag
+                flipped = (real - imag).T
+                box = folded(plus * flips[i, at, :])
+                sums[i, at, :] = plus
+                flips[i, :, at] = flipped
+                boxes[i] += box + folded(sums[i, :, at] * flipped)
+                directs[i] += folded(jnp.where(diagonal, real, 0.0))
 
     fed_group = jnp.where(core == 0, from_left, from_right)
-    fed_step = 2 + 3 * core
-    ahead_step = 2 + (3 + CHUNKS) * core
-
-    @pl.loop(0, 3 * CHUNKS + 1)
-    def _(step):
-        for q in range(SUB):
-
-            @pl.when(step < CHUNKS)
-            def _():
-                j = step * SUB + q
-                to_right(j).wait_recv()
-                over_y(j).start()
-
-                @pl.when(core == 1)
+    own_part, near_part = (0, own, group), (1, near, group)
+    fed_part, ahead_part = (2, fed, fed_group), (3, ahead, from_right)
+    nearly = PIECES - 2
+
+    @pl.when(core == 0)
+    def _():
+        @pl.loop(0, nearly)
+        def _(j):
+            to_left(j).wait_send()
+
+        @pl.loop(0, PIECES)
+        def _(j):
+            to_relay(j).start()
+
+        @pl.loop(0, PIECES)
+        def _(j):
+            to_left(j).wait_recv()
+            feed_ahead(j).start()
+
+        @pl.loop(0, PIECES)
+        def _(j):
+            feed_source(j).wait_recv()
+
+        near_copy.wait_recv()
+
+        @pl.loop(0, CHUNKS)
+        def _(n):
+            for q in range(SUB):
+                relay_core(n * SUB + q).wait_recv()
+                relay_y(n * SUB + q).wait_recv()
+            widen(n)
+            work([own_part, near_part, fed_part, ahead_part], n)
+
+    @pl.when(core == 1)
+    def _():
+        @pl.loop(0, 2 * CHUNKS)
+        def _(step):
+            for q in range(SUB):
+
+                @pl.when(step < CHUNKS)
                 def _():
+                    j = step * SUB + q
+                    to_right(j).wait_recv()
+                    over_y(j).start()
                     feed_source(j).start()
 
-            if q == 0:
-
-                @pl.when(step == fed_step)
+                @pl.when(step >= CHUNKS)
                 def _():
-                    @pl.loop(0, PIECES)
-                    def _(j):
-                        feed_ahead(j).wait_recv()
-
-                @pl.when((step >= fed_step) & (step < fed_step + CHUNKS))
-                def _():
-                    work(2, fed, fed_group, step - fed_step)
-
-            if q == 1:
-
-                @pl.when((step == ahead_step) & (core == 1))
-                def _():
-                    @pl.loop(0, PIECES)
-                    def _(j):
-                        to_left(j).wait_recv()
-
-                @pl.when((step >= ahead_step) & (step < ahead_step + CHUNKS))
-                def _():
-                    work(3, ahead, from_right, step - ahead_step)
-
-            if q == 2:
-
-                @pl.when((step == CHUNKS - 1) & (core == 1))
-                def _():
-                    @pl.loop(0, PIECES)
-                    def _(j):
-                        to_left(j).start()
-
-                @pl.when((step >= 1) & (step <= CHUNKS))
-                def _():
-                    for piece in range(SUB):
-                        over_y((step - 1) * SUB + piece).wait_recv()
-                    widen(step - 1)
-                    work(0, own, group, step - 1)
-
-            if q == 3:
-
-                @pl.when(step == 1)
-                def _():
-                    near_copy.wait_recv()
-
-                @pl.when((step >= 1) & (step <= CHUNKS))
-                def _():
-                    work(1, near, group, step - 1)
+                    j = (step - CHUNKS) * SUB + q
+                    to_relay(j).wait_recv()
+                    relay_y(j).start()
+                    relay_core(j).start()
+
+                if q == 1:
+
+                    @pl.when(step == CHUNKS - 1)
+                    def _():
+                        @pl.loop(0, nearly)
+                        def _(j):
+                            to_right(j).wait_send()
+
+                        @pl.loop(0, PIECES)
+                        def _(j):
+                            to_left(j).start()
+
+                if q == 2:
+
+                    @pl.when(step == 1)
+                    def _():
+                        near_copy.wait_recv()
+
+                    @pl.when((step >= 1) & (step <= CHUNKS))
+                    def _():
+                        for piece in range(SUB):
+                            over_y((step - 1) * SUB + piece).wait_recv()
+                        widen(step - 1)
+                        work([own_part, near_part], step - 1)
+
+                if q == 0:
+
+                    @pl.when(step == CHUNKS + 1)
+                    def _():
+                        @pl.loop(0, PIECES)
+                        def _(j):
+                            feed_ahead(j).wait_recv()
+
+                        @pl.loop(0, CHUNKS // 2)
+                        def _(n):
+                            work([fed_part], n)
+
+                    @pl.when(step == CHUNKS + 2)
+                    def _():
+                        @pl.loop(CHUNKS // 2, CHUNKS)
+                        def _(n):
+                            work([fed_part], n)
+
+        @pl.loop(0, PIECES)
+        def _(j):
+            to_left(j).wait_recv()
+
+        @pl.loop(0, CHUNKS)
+        def _(n):
+            work([ahead_part], n)
 
     separations = (1, 2 - 2 * core, 2 * core, 3)
     groups = (group, group, fed_group, from_right)
@@ -276,6 +330,35 @@
     for copy in returns:
         copy.start()
 
+    def sent():
+        @pl.when(core == 0)
+        def _():
+            @pl.loop(nearly, PIECES)
+            def _(j):
+                to_left(j).wait_send()
+
+            @pl.loop(0, PIECES)
+            def _(j):
+                to_relay(j).wait_send()
+                feed_ahead(j).wait_send()
+
+        @pl.when(core == 1)
+        def _():
+            @pl.loop(nearly, PIECES)
+            def _(j):
+                to_right(j).wait_send()
+
+            @pl.loop(0, PIECES)
+            def _(j):
+                to_left(j).wait_send()
+                over_y(j).wait_send()
+                feed_source(j).wait_send()
+                relay_y(j).wait_send()
+                relay_core(j).wait_send()
+
+        near_copy.wait_send()
+        pair_copy.wait_send()
+
     def stage(src, held, mine, places, devices, send, recv):
         copies = [
             remote(src, held.at[mine], send.at[d], recv.at[mine], device) for d, device in enumerate(devices)
@@ -283,6 +366,8 @@
         for copy in copies:
             copy.start()
         held[mine] = src[...]
+        if held is first:
+            sent()
         for d, place_of in enumerate(places):
             remote(src, held.at[place_of], send.at[d], recv.at[place_of], devices[d]).wait_recv()
         return copies, functools.reduce(jnp.add, [held[i] for i in range(held.shape[0])])
@@ -304,16 +389,6 @@
     for copy in returns + copies_1 + copies_2 + copies_3:
         copy.wait_send()
 
-    @pl.loop(0, PIECES)
-    def _(j):
-        to_right(j).wait_send()
-        to_left(j).wait_send()
-        over_y(j).wait_send()
-        feed_ahead(j).wait_send()
-
-    near_copy.wait_send()
-    pair_copy.wait_send()
-
 
 def per_device(fields, mom_pairs, deltas):
     field = (2, 2, NEV, NEV)
@@ -322,13 +397,13 @@
         trace_kernel,
         out_shape=jax.ShapeDtypeStruct((2, PAIRS, 2, SEPS), jnp.float32),
         in_specs=[
-            pl.BlockSpec(memory_space=pltpu.SMEM),
-            pl.BlockSpec(memory_space=pltpu.VMEM),
-            pl.BlockSpec(memory_space=pltpu.SMEM),
+            pl.BlockSpec(memory_space=pl.ANY),
+            pl.BlockSpec(memory_space=pl.ANY),
             pl.BlockSpec(memory_space=pl.ANY),
         ],
         out_specs=pl.BlockSpec(memory_space=pltpu.VMEM),
         scratch_shapes=[
+            pltpu.VMEM(field, jnp.bfloat16),
             pltpu.VMEM(field, jnp.bfloat16),
             pltpu.VMEM(field, jnp.bfloat16),
             pltpu.VMEM(field, jnp.bfloat16),
@@ -342,6 +417,8 @@
             pltpu.VMEM((SEPS * 8, 128), jnp.float32),
             pltpu.VMEM((2, PAIRS), jnp.int32),
             pltpu.SMEM((2, PAIRS), jnp.int32),
+            pltpu.SMEM((2, PAIRS), jnp.int32),
+            pltpu.SMEM((SEPS,), jnp.int32),
             pltpu.VMEM((8, 128), jnp.float32),
             pltpu.VMEM((2, 8, 128), jnp.float32),
             pltpu.VMEM((8, 8, 128), jnp.float32),
@@ -350,16 +427,16 @@
             pltpu.VMEM((8, 128), jnp.float32),
             pltpu.VMEM((8, 128), jnp.float32),
             dma,
-            dma((2,)),
+            dma((4,)),
             dma((2,)),
         ]
-        + [dma((PIECES,))] * 8
+        + [dma((PIECES,))] * 11
         + [dma((n,)) for n in (2, 2, 7, 8, 7, 8, 3, 4)],
         compiler_params=pltpu.CompilerParams(
             collective_id=0, has_side_effects=True, vmem_limit_bytes=62 * 1024 * 1024
         ),
         name="traces",
-    )(mom_pairs.T, mom_pairs.T, deltas, fields.reshape(field))
+    )(mom_pairs.T, deltas, fields.reshape(field))
     times, total = results.transpose(0, 2, 3, 1)
     return times[None], total
 

time: 85.9 us -> 81.8 us (0.952)
  Pallas kernels: 82.6 us -> 78.6 us
    pallas_call x1, Pallas kernels: 82.6 us -> 78.6 us  [per_device(): pl.pallas_call(trace_kernel, out_shape=jax.ShapeDtypeStruct((2, PAIRS, 2,...]
where the time goes in v4:
time: 81.8 us; the launch traced here: 80.5 us
  Pallas kernels  78.6 us (96%)
  local copies, waits for them, and re-layouts  1.26 us (2%)
    pallas_call x1, Pallas kernels, per_device(): pl.pallas_call(trace_kernel, out_shape=jax.ShapeDtypeStruct((2, PAIRS, 2,...  78.6 us

profile of v4, /device:TPU:1, one launch (start us, length us, event | category | flops | bytes accessed | tf_op | source)
XLA Modules:
  0.0 80.5 jit_solution(1902035483497009133)
XLA Ops:
  0.6 78.6 %traces.1 = f32[2,3,2,4]{3,2,1,0:T(2,128)} custom-call(s32[2,3]{1,0:T(2,128)} %bitcast.7, s32[4]{0:T(128)} %deltas_in.1, bf16[2,2,512,512]{3,2,1,0:T(8,128)(2,1)} %bitcast.5), custom_call_target="tpu_custom_call" | custom-call | tf_op jit(solution)/shard_map/traces/pallas_call | solution.py:396
  79.2 1.3 %slice_bitcast_fusion = (f32[2,4,3]{1,0,2:T(2,128)}, f32[1,2,4,3]{2,1,3,0:T(2,128)}) fusion(f32[2,2,4,3]{2,1,3,0:T(2,128)} %bitcast.6), kind=kLoop, calls=%fused_computation | loop fusion | bytes 384 | tf_op jit(solution)/shard_map/unstack | solution.py:440

commit v5 on v4

--- a/solution.py
+++ b/solution.py
@@ -11,6 +11,7 @@
 CHIPS_PER_PLANE = 32
 ROWS = 128
 CHUNKS = 4
+LEVELS, LEVEL_DEVICES = 8, 32
 SUB = 4
 PIECES = CHUNKS * SUB
 PIECE_ROWS = ROWS // SUB
@@ -41,79 +42,81 @@
 def trace_kernel(
     pairs, deltas_in, fields, results,
     own, near, fed, ahead, relay, source, wide, sums, flips, boxes, directs, rows_out, pairs_in, pairs_own, pairs_other, deltas,
-    tile, back, first, second, third, after_first, after_second, load_sem, pair_sems, near_sems, send_right, recv_right, send_left, recv_left, send_y, recv_y, send_core, recv_core,
-    recv_relay, relay_sent_y, relay_sent_core,
-    back_send, back_recv, send_1, recv_1, send_2, recv_2, send_3, recv_3,
+    tile, back, first, second, after_first, load_sem, pair_sems, near_sems, first_sent, passed,
+    recv_right, recv_relay, recv_left, recv_y, recv_core, recv_fed, stage_sems,
 ):
     time, group, core, right, left, across, partner = place()
     count = lax.axis_size("tm")
     from_left = left["mom"]
     from_right = right["mom"]
 
-    def rows(j):
-        return pl.ds(pl.multiple_of(j * PIECE_ROWS, PIECE_ROWS), PIECE_ROWS)
+    def rows(j, count_of=1):
+        return pl.ds(pl.multiple_of(j * PIECE_ROWS, PIECE_ROWS), PIECE_ROWS * count_of)
 
     def remote(src, dst, send, recv, device):
         return pltpu.make_async_remote_copy(
             src_ref=src, dst_ref=dst, send_sem=send, recv_sem=recv, device_id=device, device_id_type=MESH
         )
 
-    def to_right(j, held=own):
+    def to_right(j, held=own, sent=0, many=1):
+        at = rows(j, many)
         return remote(
-            held.at[:, :, rows(j), :], source.at[group, :, :, rows(j), :], send_right.at[j], recv_right.at[j], right
+            held.at[:, :, at, :], source.at[group, :, :, at, :], first_sent.at[sent], recv_right.at[j], right
         )
 
-    def to_left(j, held=own):
-        return remote(held.at[:, :, rows(j), :], ahead.at[:, :, rows(j), :], send_left.at[j], recv_left.at[j], left)
-
-    def to_relay(j):
+    def to_left(j, held=own, sent=0, many=1):
+        at = rows(j, many)
+        return remote(held.at[:, :, at, :], ahead.at[:, :, at, :], first_sent.at[sent], recv_left.at[j // SUB], left)
+
+    def to_relay(j, many=1):
+        at = rows(j, many)
         device = {"tm": (time + 3) % count, "mom": right["mom"]}
+        return remote(own.at[:, :, at, :], relay.at[:, :, at, :], first_sent.at[2], recv_relay.at[j], device)
+
+    def relay_y(j, many=1):
+        at = rows(j, many)
+        device = {"tm": partner["tm"], "mom": 1 - group}
         return remote(
-            own.at[:, :, rows(j), :], relay.at[:, :, rows(j), :], send_right.at[j], recv_relay.at[j], device
+            relay.at[:, :, at, :], source.at[from_left, :, :, at, :], passed.at[0], recv_y.at[j // SUB], device
         )
 
-    def relay_y(j):
-        part = source.at[from_left, :, :, rows(j), :]
-        device = {"tm": partner["tm"], "mom": 1 - group}
-        return remote(relay.at[:, :, rows(j), :], part, relay_sent_y.at[j], recv_y.at[j], device)
-
-    def relay_core(j):
-        part = source.at[from_left, :, :, rows(j), :]
-        return remote(relay.at[:, :, rows(j), :], part, relay_sent_core.at[j], recv_right.at[j], partner)
-
-    def over_y(j):
-        part = source.at[from_left, :, :, rows(j), :]
-        return remote(part, part, send_y.at[j], recv_y.at[j], across)
-
-    def feed_source(j):
+    def relay_core(j, many=1):
+        at = rows(j, many)
         return remote(
-            source.at[from_left, :, :, rows(j), :], fed.at[:, :, rows(j), :], send_core.at[j], recv_core.at[j], partner
+            relay.at[:, :, at, :], source.at[from_left, :, :, at, :], passed.at[1], recv_core.at[j // SUB], partner
         )
 
-    def feed_ahead(j):
-        return remote(ahead.at[:, :, rows(j), :], fed.at[:, :, rows(j), :], send_core.at[j], recv_core.at[j], partner)
-
+    def over_y(j, many=1):
+        part = source.at[from_left, :, :, rows(j, many), :]
+        return remote(part, part, passed.at[2], recv_y.at[j // SUB], across)
+
+    def feed_source(j, many=1):
+        at = rows(j, many)
+        return remote(source.at[from_left, :, :, at, :], fed.at[:, :, at, :], passed.at[3], recv_fed.at[0], partner)
+
+    def feed_ahead(j, many=1):
+        at = rows(j, many)
+        return remote(ahead.at[:, :, at, :], fed.at[:, :, at, :], passed.at[3], recv_fed.at[0], partner)
+
+    nearly = PIECES - SUB // 2
     near_copy = remote(fields, near, near_sems.at[0], near_sems.at[1], partner)
     pair_copy = remote(pairs, pairs_in, pair_sems.at[0], pair_sems.at[1], across)
     load = pltpu.make_async_copy(fields, own, load_sem)
 
-    row, level, plane = time % 8, time // 8 % 8, time // 64
-    in_row = [(row + d) % 8 for d in range(1, 8)]
-    in_column = [(level + d) % 8 for d in range(1, 8)]
-    corner = plane * 2 + group
-    in_plane = [(corner + d) % 4 for d in range(1, 4)]
-    row_devices = [{"tm": time - row + r, "mom": group} for r in in_row]
-    column_devices = [{"tm": time + (r - level) * 8, "mom": group} for r in in_column]
-    plane_devices = [{"tm": time + (r // 2 - plane) * 64, "mom": r % 2} for r in in_plane]
+    level = time // 8 % 8
+    place_in_level = (time // 64 * 2 + group) * 8 + time % 8
+    in_level = [(place_in_level + d) % LEVEL_DEVICES for d in range(1, LEVEL_DEVICES)]
+    in_column = [(level + d) % LEVELS for d in range(1, LEVELS)]
+    level_devices = [{"tm": n // 16 * 64 + level * 8 + n % 8, "mom": n // 8 % 2} for n in in_level]
+    column_devices = [{"tm": time + (n - level) * 8, "mom": group} for n in in_column]
     back_devices = [{"tm": (time + count - 2) % count, "mom": h} for h in range(2)]
     behind_devices = [{"tm": (time + 2) % count, "mom": h} for h in range(2)]
 
     barrier = pltpu.get_barrier_semaphore()
     relays = [
-        {"tm": partner["tm"], "mom": 1 - group},
         {"tm": (time + count + 3 - 6 * core) % count, "mom": jnp.where(core == 0, right["mom"], left["mom"])},
     ]
-    greeted = column_devices + plane_devices + row_devices + back_devices + behind_devices + relays
+    greeted = column_devices + level_devices + back_devices + behind_devices + relays
     for device in greeted:
         pl.semaphore_signal(barrier, inc=1, device_id=device, device_id_type=MESH)
     own_tables = [
@@ -129,13 +132,13 @@
     def _():
         @pl.loop(0, PIECES)
         def _(j):
-            to_right(j, fields).start()
+            to_right(j, fields, j // nearly).start()
 
     @pl.when(core == 0)
     def _():
         @pl.loop(0, PIECES)
         def _(j):
-            to_left(j, fields).start()
+            to_left(j, fields, j // nearly).start()
 
     pair_copy.start()
     near_copy.start()
@@ -199,34 +202,27 @@
     fed_group = jnp.where(core == 0, from_left, from_right)
     own_part, near_part = (0, own, group), (1, near, group)
     fed_part, ahead_part = (2, fed, fed_group), (3, ahead, from_right)
-    nearly = PIECES - 2
 
     @pl.when(core == 0)
     def _():
-        @pl.loop(0, nearly)
-        def _(j):
-            to_left(j).wait_send()
+        to_left(0, many=nearly).wait_send()
 
         @pl.loop(0, PIECES)
         def _(j):
             to_relay(j).start()
 
-        @pl.loop(0, PIECES)
-        def _(j):
-            to_left(j).wait_recv()
-            feed_ahead(j).start()
-
-        @pl.loop(0, PIECES)
-        def _(j):
-            feed_source(j).wait_recv()
-
-        near_copy.wait_recv()
-
         @pl.loop(0, CHUNKS)
         def _(n):
-            for q in range(SUB):
-                relay_core(n * SUB + q).wait_recv()
-                relay_y(n * SUB + q).wait_recv()
+            to_left(n * SUB, many=SUB).wait_recv()
+            feed_ahead(n * SUB, SUB).start()
+
+        feed_source(0, PIECES).wait_recv()
+        near_copy.wait_recv()
+
+        @pl.loop(0, CHUNKS)
+        def _(n):
+            relay_core(n * SUB, SUB).wait_recv()
+            relay_y(n * SUB, SUB).wait_recv()
             widen(n)
             work([own_part, near_part, fed_part, ahead_part], n)
 
@@ -254,13 +250,11 @@
 
                     @pl.when(step == CHUNKS - 1)
                     def _():
-                        @pl.loop(0, nearly)
-                        def _(j):
-                            to_right(j).wait_send()
+                        to_right(0, many=nearly).wait_send()
 
                         @pl.loop(0, PIECES)
                         def _(j):
-                            to_left(j).start()
+                            to_left(j, sent=2).start()
 
                 if q == 2:
 
@@ -270,8 +264,7 @@
 
                     @pl.when((step >= 1) & (step <= CHUNKS))
                     def _():
-                        for piece in range(SUB):
-                            over_y((step - 1) * SUB + piece).wait_recv()
+                        over_y((step - 1) * SUB, SUB).wait_recv()
                         widen(step - 1)
                         work([own_part, near_part], step - 1)
 
@@ -279,9 +272,7 @@
 
                     @pl.when(step == CHUNKS + 1)
                     def _():
-                        @pl.loop(0, PIECES)
-                        def _(j):
-                            feed_ahead(j).wait_recv()
+                        feed_ahead(0, PIECES).wait_recv()
 
                         @pl.loop(0, CHUNKS // 2)
                         def _(n):
@@ -293,9 +284,9 @@
                         def _(n):
                             work([fed_part], n)
 
-        @pl.loop(0, PIECES)
-        def _(j):
-            to_left(j).wait_recv()
+        @pl.loop(0, CHUNKS)
+        def _(n):
+            to_left(n * SUB, many=SUB).wait_recv()
 
         @pl.loop(0, CHUNKS)
         def _(n):
@@ -324,8 +315,7 @@
     )
 
     returns = [
-        remote(tile, back.at[group], back_send.at[h], back_recv.at[group], device)
-        for h, device in enumerate(back_devices)
+        remote(tile, back.at[group], stage_sems.at[0], stage_sems.at[1], device) for device in back_devices
     ]
     for copy in returns:
         copy.start()
@@ -333,61 +323,47 @@
     def sent():
         @pl.when(core == 0)
         def _():
-            @pl.loop(nearly, PIECES)
-            def _(j):
-                to_left(j).wait_send()
-
-            @pl.loop(0, PIECES)
-            def _(j):
-                to_relay(j).wait_send()
-                feed_ahead(j).wait_send()
+            to_left(nearly, sent=1, many=PIECES - nearly).wait_send()
+            to_relay(0, PIECES).wait_send()
+            feed_ahead(0, PIECES).wait_send()
 
         @pl.when(core == 1)
         def _():
-            @pl.loop(nearly, PIECES)
-            def _(j):
-                to_right(j).wait_send()
-
-            @pl.loop(0, PIECES)
-            def _(j):
-                to_left(j).wait_send()
-                over_y(j).wait_send()
-                feed_source(j).wait_send()
-                relay_y(j).wait_send()
-                relay_core(j).wait_send()
+            to_right(nearly, sent=1, many=PIECES - nearly).wait_send()
+            to_left(0, sent=2, many=PIECES).wait_send()
+            over_y(0, PIECES).wait_send()
+            feed_source(0, PIECES).wait_send()
+            relay_y(0, PIECES).wait_send()
+            relay_core(0, PIECES).wait_send()
 
         near_copy.wait_send()
         pair_copy.wait_send()
 
-    def stage(src, held, mine, places, devices, send, recv):
-        copies = [
-            remote(src, held.at[mine], send.at[d], recv.at[mine], device) for d, device in enumerate(devices)
-        ]
-        for copy in copies:
-            copy.start()
+    def stage(src, held, mine, devices, sems):
+        for device in devices:
+            remote(src, held.at[mine], stage_sems.at[sems], stage_sems.at[sems + 1], device).start()
         held[mine] = src[...]
         if held is first:
             sent()
-        for d, place_of in enumerate(places):
-            remote(src, held.at[place_of], send.at[d], recv.at[place_of], devices[d]).wait_recv()
-        return copies, functools.reduce(jnp.add, [held[i] for i in range(held.shape[0])])
+        arrived = held.at[: len(devices)]
+        all_of_them = remote(arrived, arrived, stage_sems.at[sems], stage_sems.at[sems + 1], devices[0])
+        all_of_them.wait_recv()
+        return all_of_them, functools.reduce(jnp.add, [held[i] for i in range(held.shape[0])])
 
     def deliver(values, out):
         mine = jnp.where(group == 0, values[:, :SEPS], values[:, SEPS : 2 * SEPS])
         for which in range(PAIRS):
             results[out, which] = mine[which * 2 : which * 2 + 2]
 
-    copies_1, value = stage(tile, first, row, in_row, row_devices, send_1, recv_1)
+    copies_1, value = stage(tile, first, place_in_level, level_devices, 2)
     after_first[...] = value
-    copies_2, value = stage(after_first, second, level, in_column, column_devices, send_2, recv_2)
-    after_second[...] = value
-    copies_3, value = stage(after_second, third, corner, in_plane, plane_devices, send_3, recv_3)
+    copies_2, value = stage(after_first, second, level, column_devices, 4)
     deliver(value, 1)
-    for h in range(2):
-        remote(tile, back.at[h], back_send.at[h], back_recv.at[h], back_devices[h]).wait_recv()
+    both = remote(back, back, stage_sems.at[0], stage_sems.at[1], back_devices[0])
+    both.wait_recv()
     deliver(back[0] + back[1], 0)
-    for copy in returns + copies_1 + copies_2 + copies_3:
-        copy.wait_send()
+    for copies in (both, copies_1, copies_2):
+        copies.wait_send()
 
 
 def per_device(fields, mom_pairs, deltas):
@@ -395,7 +371,7 @@
     dma = pltpu.SemaphoreType.DMA
     results = pl.pallas_call(
         trace_kernel,
-        out_shape=jax.ShapeDtypeStruct((2, PAIRS, 2, SEPS), jnp.float32),
+        out_shape=pltpu.VMEM((2, PAIRS, 2, SEPS), jnp.float32),
         in_specs=[
             pl.BlockSpec(memory_space=pl.ANY),
             pl.BlockSpec(memory_space=pl.ANY),
@@ -421,17 +397,12 @@
             pltpu.SMEM((SEPS,), jnp.int32),
             pltpu.VMEM((8, 128), jnp.float32),
             pltpu.VMEM((2, 8, 128), jnp.float32),
-            pltpu.VMEM((8, 8, 128), jnp.float32),
-            pltpu.VMEM((8, 8, 128), jnp.float32),
-            pltpu.VMEM((4, 8, 128), jnp.float32),
-            pltpu.VMEM((8, 128), jnp.float32),
+            pltpu.VMEM((LEVEL_DEVICES, 8, 128), jnp.float32),
+            pltpu.VMEM((LEVELS, 8, 128), jnp.float32),
             pltpu.VMEM((8, 128), jnp.float32),
             dma,
-            dma((4,)),
-            dma((2,)),
         ]
-        + [dma((PIECES,))] * 11
-        + [dma((n,)) for n in (2, 2, 7, 8, 7, 8, 3, 4)],
+        + [dma((n,)) for n in (4, 2, 3, 4, PIECES, PIECES, CHUNKS, CHUNKS, CHUNKS, 1, 6)],
         compiler_params=pltpu.CompilerParams(
             collective_id=0, has_side_effects=True, vmem_limit_bytes=62 * 1024 * 1024
         ),

time: 81.8 us -> 77.8 us (0.951); the launches traced: 80.5 us -> 77.7 us
  Pallas kernels: 78.6 us -> 76.5 us
    pallas_call x1, Pallas kernels: 78.6 us -> 76.5 us  [per_device(): pl.pallas_call(trace_kernel, out_shape=pltpu.VMEM((2, PAIRS, 2, SEPS), jn...]
where the time goes in v5:
time: 77.8 us; the launch traced here: 77.7 us
  Pallas kernels  76.5 us (98%)
    pallas_call x1, Pallas kernels, per_device(): pl.pallas_call(trace_kernel, out_shape=pltpu.VMEM((2, PAIRS, 2, SEPS), jn...  76.5 us

profile of v5, /device:TPU:1, one launch (start us, length us, event | category | flops | bytes accessed | tf_op | source)
XLA Modules:
  0.0 77.7 jit_solution(12588162250609138767)
XLA Ops:
  0.6 76.5 %traces.1 = f32[2,3,2,4]{3,2,1,0:T(2,128)S(1)} custom-call(s32[2,3]{1,0:T(2,128)} %bitcast.7, s32[4]{0:T(128)} %deltas_in.1, bf16[2,2,512,512]{3,2,1,0:T(8,128)(2,1)} %bitcast.6), custom_call_target="tpu_custom_call" | custom-call | tf_op jit(solution)/shard_map/traces/pallas_call | solution.py:372
  77.1 0.6 slice_bitcast_fusion

commit v6 on v5

--- a/solution.py
+++ b/solution.py
@@ -41,9 +41,9 @@
 
 def trace_kernel(
     pairs, deltas_in, fields, results,
-    own, near, fed, ahead, relay, source, wide, sums, flips, boxes, directs, rows_out, pairs_in, pairs_own, pairs_other, deltas,
+    own, near, fed, ahead, relay, spare, relay_spare, source, wide, sums, flips, boxes, directs, rows_out, pairs_in, pairs_own, pairs_other, deltas,
     tile, back, first, second, after_first, load_sem, pair_sems, near_sems, first_sent, passed,
-    recv_right, recv_relay, recv_left, recv_y, recv_core, recv_fed, stage_sems,
+    recv_right, recv_relay, recv_left, recv_y, recv_core, recv_fed, stage_sems, spare_sems,
 ):
     time, group, core, right, left, across, partner = place()
     count = lax.axis_size("tm")
@@ -58,15 +58,15 @@
             src_ref=src, dst_ref=dst, send_sem=send, recv_sem=recv, device_id=device, device_id_type=MESH
         )
 
-    def to_right(j, held=own, sent=0, many=1):
+    def to_right(j, sent=0, many=1):
         at = rows(j, many)
         return remote(
-            held.at[:, :, at, :], source.at[group, :, :, at, :], first_sent.at[sent], recv_right.at[j], right
+            own.at[:, :, at, :], source.at[group, :, :, at, :], first_sent.at[sent], recv_right.at[j], right
         )
 
-    def to_left(j, held=own, sent=0, many=1):
-        at = rows(j, many)
-        return remote(held.at[:, :, at, :], ahead.at[:, :, at, :], first_sent.at[sent], recv_left.at[j // SUB], left)
+    def to_left(j, sent=0, many=1):
+        at = rows(j, many)
+        return remote(own.at[:, :, at, :], ahead.at[:, :, at, :], first_sent.at[sent], recv_left.at[j // SUB], left)
 
     def to_relay(j, many=1):
         at = rows(j, many)
@@ -99,7 +99,15 @@
         return remote(ahead.at[:, :, at, :], fed.at[:, :, at, :], passed.at[3], recv_fed.at[0], partner)
 
     nearly = PIECES - SUB // 2
-    near_copy = remote(fields, near, near_sems.at[0], near_sems.at[1], partner)
+    last = PIECES - 1
+    spare_copy = remote(own.at[:, :, rows(last), :], spare, spare_sems.at[0], spare_sems.at[1], across)
+    spare_right = remote(
+        spare, relay_spare, spare_sems.at[2], spare_sems.at[3], {"tm": (time + 3) % count, "mom": right["mom"]}
+    )
+    spare_core = remote(
+        relay_spare, source.at[1 - from_left, :, :, rows(last), :], spare_sems.at[4], spare_sems.at[5], partner
+    )
+    near_copy = remote(own, near, near_sems.at[0], near_sems.at[1], partner)
     pair_copy = remote(pairs, pairs_in, pair_sems.at[0], pair_sems.at[1], across)
     load = pltpu.make_async_copy(fields, own, load_sem)
 
@@ -126,19 +134,22 @@
     load.start()
     for copy in own_tables:
         copy.start()
+    load.wait()
     pl.semaphore_wait(barrier, len(greeted))
 
     @pl.when(core == 1)
     def _():
         @pl.loop(0, PIECES)
         def _(j):
-            to_right(j, fields, j // nearly).start()
+            to_right(j, j // nearly).start()
 
     @pl.when(core == 0)
     def _():
         @pl.loop(0, PIECES)
         def _(j):
-            to_left(j, fields, j // nearly).start()
+            to_left(j, j // nearly).start()
+
+        spare_copy.start()
 
     pair_copy.start()
     near_copy.start()
@@ -155,7 +166,6 @@
             flips[i, at, :] = jnp.zeros((32, NEV), jnp.float32)
 
     rows_out[...] = jnp.zeros_like(rows_out)
-    load.wait()
     for copy in own_tables:
         copy.wait()
     pair_copy.wait_recv()
@@ -211,6 +221,9 @@
         def _(j):
             to_relay(j).start()
 
+        spare_copy.wait_recv()
+        spare_right.start()
+
         @pl.loop(0, CHUNKS)
         def _(n):
             to_left(n * SUB, many=SUB).wait_recv()
@@ -222,7 +235,16 @@
         @pl.loop(0, CHUNKS)
         def _(n):
             relay_core(n * SUB, SUB).wait_recv()
-            relay_y(n * SUB, SUB).wait_recv()
+
+            @pl.when(n < CHUNKS - 1)
+            def _():
+                relay_y(n * SUB, SUB).wait_recv()
+
+            @pl.when(n == CHUNKS - 1)
+            def _():
+                relay_y(last + 1 - SUB, SUB - 1).wait_recv()
+                spare_core.wait_recv()
+
             widen(n)
             work([own_part, near_part, fed_part, ahead_part], n)
 
@@ -243,8 +265,11 @@
                 def _():
                     j = (step - CHUNKS) * SUB + q
                     to_relay(j).wait_recv()
-                    relay_y(j).start()
                     relay_core(j).start()
+
+                    @pl.when(j < last)
+                    def _():
+                        relay_y(j).start()
 
                 if q == 1:
 
@@ -283,6 +308,9 @@
                         @pl.loop(CHUNKS // 2, CHUNKS)
                         def _(n):
                             work([fed_part], n)
+
+        spare_right.wait_recv()
+        spare_core.start()
 
         @pl.loop(0, CHUNKS)
         def _(n):
@@ -325,6 +353,8 @@
         def _():
             to_left(nearly, sent=1, many=PIECES - nearly).wait_send()
             to_relay(0, PIECES).wait_send()
+            spare_copy.wait_send()
+            spare_right.wait_send()
             feed_ahead(0, PIECES).wait_send()
 
         @pl.when(core == 1)
@@ -333,7 +363,8 @@
             to_left(0, sent=2, many=PIECES).wait_send()
             over_y(0, PIECES).wait_send()
             feed_source(0, PIECES).wait_send()
-            relay_y(0, PIECES).wait_send()
+            relay_y(0, last).wait_send()
+            spare_core.wait_send()
             relay_core(0, PIECES).wait_send()
 
         near_copy.wait_send()
@@ -384,6 +415,8 @@
             pltpu.VMEM(field, jnp.bfloat16),
             pltpu.VMEM(field, jnp.bfloat16),
             pltpu.VMEM(field, jnp.bfloat16),
+            pltpu.VMEM((2, 2, PIECE_ROWS, NEV), jnp.bfloat16),
+            pltpu.VMEM((2, 2, PIECE_ROWS, NEV), jnp.bfloat16),
             pltpu.VMEM((2, *field), jnp.bfloat16),
             pltpu.VMEM((4, CHUNKS, 2 * ROWS, 2 * NEV), jnp.bfloat16),
             pltpu.VMEM((SEPS * PAIRS, NEV, NEV), jnp.float32),
@@ -402,7 +435,7 @@
             pltpu.VMEM((8, 128), jnp.float32),
             dma,
         ]
-        + [dma((n,)) for n in (4, 2, 3, 4, PIECES, PIECES, CHUNKS, CHUNKS, CHUNKS, 1, 6)],
+        + [dma((n,)) for n in (4, 2, 3, 4, PIECES, PIECES, CHUNKS, CHUNKS, CHUNKS, 1, 6, 6)],
         compiler_params=pltpu.CompilerParams(
             collective_id=0, has_side_effects=True, vmem_limit_bytes=62 * 1024 * 1024
         ),

time: 77.8 us -> 76.4 us (0.982)
  Pallas kernels: 76.5 us -> 75 us
    pallas_call x1, Pallas kernels: 76.5 us -> 75 us  [per_device(): pl.pallas_call(trace_kernel, out_shape=pltpu.VMEM((2, PAIRS, 2, SEPS), jn...]
where the time goes in v6:
time: 76.4 us; the launch traced here: 76.3 us
  Pallas kernels  75 us (98%)
    pallas_call x1, Pallas kernels, per_device(): pl.pallas_call(trace_kernel, out_shape=pltpu.VMEM((2, PAIRS, 2, SEPS), jn...  75 us

profile of v6, /device:TPU:1, one launch (start us, length us, event | category | flops | bytes accessed | tf_op | source)
XLA Modules:
  0.0 76.3 jit_solution(17607698231954910735)
XLA Ops:
  0.6 75.0 %traces.1 = f32[2,3,2,4]{3,2,1,0:T(2,128)S(1)} custom-call(s32[2,3]{1,0:T(2,128)} %bitcast.7, s32[4]{0:T(128)} %deltas_in.1, bf16[2,2,512,512]{3,2,1,0:T(8,128)(2,1)} %bitcast.6), custom_call_target="tpu_custom_call" | custom-call | tf_op jit(solution)/shard_map/traces/pallas_call | solution.py:403
  75.7 0.6 slice_bitcast_fusion

commit v7 on v6

--- a/solution.py
+++ b/solution.py
@@ -299,15 +299,11 @@
                     def _():
                         feed_ahead(0, PIECES).wait_recv()
 
+                    @pl.when((step == CHUNKS + 1) | (step == CHUNKS + 2))
+                    def _():
                         @pl.loop(0, CHUNKS // 2)
                         def _(n):
-                            work([fed_part], n)
-
-                    @pl.when(step == CHUNKS + 2)
-                    def _():
-                        @pl.loop(CHUNKS // 2, CHUNKS)
-                        def _(n):
-                            work([fed_part], n)
+                            work([fed_part], (step - CHUNKS - 1) * (CHUNKS // 2) + n)
 
         spare_right.wait_recv()
         spare_core.start()
@@ -316,13 +312,13 @@
         def _(n):
             to_left(n * SUB, many=SUB).wait_recv()
 
-        @pl.loop(0, CHUNKS)
-        def _(n):
+        for n in range(CHUNKS):
             work([ahead_part], n)
 
     separations = (1, 2 - 2 * core, 2 * core, 3)
     groups = (group, group, fed_group, from_right)
     lane = lax.broadcasted_iota(jnp.int32, (8, 128), 1)
+    sublane = lax.broadcasted_iota(jnp.int32, (8, 128), 0)
     wanted = functools.reduce(
         jnp.add, [jnp.where(lane % SEPS == r, deltas[r], 0) for r in range(SEPS)]
     )
@@ -332,15 +328,18 @@
                 line = slot * 8 + which * 2 + kind
                 rows_out[line : line + 1, :] = values[slot * PAIRS + which].sum(0, keepdims=True)
     totals = jnp.broadcast_to(rows_out[...].sum(1, keepdims=True), rows_out.shape)
-    tile[...] = functools.reduce(
+    placed = functools.reduce(
         jnp.add,
         [
             jnp.where(
-                (wanted == separations[slot]) & (lane // SEPS == groups[slot]), totals[slot * 8 : slot * 8 + 8], 0.0
+                (wanted == separations[slot]) & (lane // SEPS % 2 == groups[slot]) & (lane // (2 * SEPS) == sublane),
+                totals[slot * 8 : slot * 8 + 8],
+                0.0,
             )
             for slot in range(SEPS)
         ],
     )
+    tile[...] = placed.sum(0, keepdims=True)
 
     returns = [
         remote(tile, back.at[group], stage_sems.at[0], stage_sems.at[1], device) for device in back_devices
@@ -382,9 +381,11 @@
         return all_of_them, functools.reduce(jnp.add, [held[i] for i in range(held.shape[0])])
 
     def deliver(values, out):
-        mine = jnp.where(group == 0, values[:, :SEPS], values[:, SEPS : 2 * SEPS])
         for which in range(PAIRS):
-            results[out, which] = mine[which * 2 : which * 2 + 2]
+            for kind in range(2):
+                begin = (which * 2 + kind) * 2 * SEPS
+                both_groups = values[:, begin : begin + SEPS], values[:, begin + SEPS : begin + 2 * SEPS]
+                results[out, which, kind : kind + 1, :] = jnp.where(group == 0, *both_groups)
 
     copies_1, value = stage(tile, first, place_in_level, level_devices, 2)
     after_first[...] = value
@@ -428,11 +429,11 @@
             pltpu.SMEM((2, PAIRS), jnp.int32),
             pltpu.SMEM((2, PAIRS), jnp.int32),
             pltpu.SMEM((SEPS,), jnp.int32),
-            pltpu.VMEM((8, 128), jnp.float32),
-            pltpu.VMEM((2, 8, 128), jnp.float32),
-            pltpu.VMEM((LEVEL_DEVICES, 8, 128), jnp.float32),
-            pltpu.VMEM((LEVELS, 8, 128), jnp.float32),
-            pltpu.VMEM((8, 128), jnp.float32),
+            pltpu.VMEM((1, 128), jnp.float32),
+            pltpu.VMEM((2, 1, 128), jnp.float32),
+            pltpu.VMEM((LEVEL_DEVICES, 1, 128), jnp.float32),
+            pltpu.VMEM((LEVELS, 1, 128), jnp.float32),
+            pltpu.VMEM((1, 128), jnp.float32),
             dma,
         ]
         + [dma((n,)) for n in (4, 2, 3, 4, PIECES, PIECES, CHUNKS, CHUNKS, CHUNKS, 1, 6, 6)],

time: 76.4 us -> 75.8 us (level)
  no operation moved by 1% of the time
where the time goes in v7:
time: 75.8 us; the launch traced here: 75.7 us
  Pallas kernels  74.5 us (98%)
    pallas_call x1, Pallas kernels, per_device(): pl.pallas_call(trace_kernel, out_shape=pltpu.VMEM((2, PAIRS, 2, SEPS), jn...  74.5 us

profile of v7, /device:TPU:1, one launch (start us, length us, event | category | flops | bytes accessed | tf_op | source)
XLA Modules:
  0.0 75.7 jit_solution(15517231728937714284)
XLA Ops:
  0.6 74.5 %traces.1 = f32[2,3,2,4]{3,2,1,0:T(2,128)S(1)} custom-call(s32[2,3]{1,0:T(2,128)} %bitcast.7, s32[4]{0:T(128)} %deltas_in.1, bf16[2,2,512,512]{3,2,1,0:T(8,128)(2,1)} %bitcast.6), custom_call_target="tpu_custom_call" | custom-call | tf_op jit(solution)/shard_map/traces/pallas_call | solution.py:404
  75.2 0.6 slice_bitcast_fusion

commit v8 on v7

--- a/solution.py
+++ b/solution.py
@@ -271,7 +271,7 @@
                     def _():
                         relay_y(j).start()
 
-                if q == 1:
+                if q == 0:
 
                     @pl.when(step == CHUNKS - 1)
                     def _():

time: 75.8 us -> 76.4 us (level)
  no operation moved by 1% of the time
where the time goes in v8:
time: 76.4 us; the launch traced here: 76.2 us
  Pallas kernels  75 us (98%)
    pallas_call x1, Pallas kernels, per_device(): pl.pallas_call(trace_kernel, out_shape=pltpu.VMEM((2, PAIRS, 2, SEPS), jn...  75 us

profile of v8, /device:TPU:1, one launch (start us, length us, event | category | flops | bytes accessed | tf_op | source)
XLA Modules:
  0.0 76.2 jit_solution(16400610377231249445)
XLA Ops:
  0.6 75.0 %traces.1 = f32[2,3,2,4]{3,2,1,0:T(2,128)S(1)} custom-call(s32[2,3]{1,0:T(2,128)} %bitcast.7, s32[4]{0:T(128)} %deltas_in.1, bf16[2,2,512,512]{3,2,1,0:T(8,128)(2,1)} %bitcast.6), custom_call_target="tpu_custom_call" | custom-call | tf_op jit(solution)/shard_map/traces/pallas_call | solution.py:404
  75.7 0.6 slice_bitcast_fusion

commit v9 on v8

--- a/solution.py
+++ b/solution.py
@@ -107,6 +107,7 @@
     spare_core = remote(
         relay_spare, source.at[1 - from_left, :, :, rows(last), :], spare_sems.at[4], spare_sems.at[5], partner
     )
+    soon = PIECES - SUB
     near_copy = remote(own, near, near_sems.at[0], near_sems.at[1], partner)
     pair_copy = remote(pairs, pairs_in, pair_sems.at[0], pair_sems.at[1], across)
     load = pltpu.make_async_copy(fields, own, load_sem)
@@ -141,7 +142,7 @@
     def _():
         @pl.loop(0, PIECES)
         def _(j):
-            to_right(j, j // nearly).start()
+            to_right(j, j // soon).start()
 
     @pl.when(core == 0)
     def _():
@@ -275,7 +276,7 @@
 
                     @pl.when(step == CHUNKS - 1)
                     def _():
-                        to_right(0, many=nearly).wait_send()
+                        to_right(0, many=soon).wait_send()
 
                         @pl.loop(0, PIECES)
                         def _(j):
@@ -358,7 +359,7 @@
 
         @pl.when(core == 1)
         def _():
-            to_right(nearly, sent=1, many=PIECES - nearly).wait_send()
+            to_right(soon, sent=1, many=PIECES - soon).wait_send()
             to_left(0, sent=2, many=PIECES).wait_send()
             over_y(0, PIECES).wait_send()
             feed_source(0, PIECES).wait_send()

time: 76.4 us -> 76.4 us (level)
  no operation moved by 1% of the time
where the time goes in v9:
time: 76.4 us; the launch traced here: 76.2 us
  Pallas kernels  75 us (98%)
    pallas_call x1, Pallas kernels, per_device(): pl.pallas_call(trace_kernel, out_shape=pltpu.VMEM((2, PAIRS, 2, SEPS), jn...  75 us

profile of v9, /device:TPU:1, one launch (start us, length us, event | category | flops | bytes accessed | tf_op | source)
XLA Modules:
  0.0 76.2 jit_solution(7750179764134166504)
XLA Ops:
  0.6 75.0 %traces.1 = f32[2,3,2,4]{3,2,1,0:T(2,128)S(1)} custom-call(s32[2,3]{1,0:T(2,128)} %bitcast.7, s32[4]{0:T(128)} %deltas_in.1, bf16[2,2,512,512]{3,2,1,0:T(8,128)(2,1)} %bitcast.6), custom_call_target="tpu_custom_call" | custom-call | tf_op jit(solution)/shard_map/traces/pallas_call | solution.py:405
  75.7 0.6 slice_bitcast_fusion
